TPU v7x, 512 devices: a 4x2x32 block of a 4x8x32 slice. The times are simulated.
512 devices in a mesh: rep: 2 (over y), tp: 32 (over z), ep: 8 (over x, core).
Axes of the slice: x: 4, y: 2, z: 32, core: 2. Of those that a mesh axis runs over, the one named last changes fastest.
The devices are a block of a 4x8x32 slice.
Arguments:
- tokens: bfloat16 [1536, 3072], P(('rep', 'ep'), 'tp'), parts along dimension 0, may hold values from -6 to 6
- routing: int32 [1536, 2], P(('rep', 'ep')), parts along dimension 0, may hold values from 0 to 7, all different within a row; in each aligned block of 96 rows (0 to 95, 96 to 191, ...) at most 30 rows name the same one
- route_gates: float32 [1536, 2], P(('rep', 'ep')), parts along dimension 0, may hold values from 0.2 to 1
- expert_gate: bfloat16 [8, 3072, 8192], P('ep', None, 'tp'), may hold values from -0.109375 to 0.109375
- expert_up: bfloat16 [8, 3072, 8192], P('ep', None, 'tp'), may hold values from -0.109375 to 0.109375
- expert_down: bfloat16 [8, 8192, 3072], P('ep', 'tp'), may hold values from -0.0625 to 0.0625
Outputs:
- mixture: bfloat16 [1536, 3072], P(('rep', 'ep'), 'tp'), parts along dimension 0
There are 2 independent parts, one for each index of `rep`. A program takes and returns all parts, laid end to end along the dimension named above; an argument that names none is the same for every part. Nothing has to cross between parts.
Inputs may be any that keep to these rules, and one draw needn't show every extreme that they name: `routing`: each token names two different experts. In each aligned block of 96 tokens (the rows of one index of ep) no expert is named by more than 30 tokens, a bound that some block reaches.
All inputs are finite; a program needn't handle non-finite values.
Results may differ from a plain program's by a relative error of at most 0.0085.
Values may be sent and summed in bfloat16 or wider, within the bound.
No kernel may reach another device: no remote copies, remote signals or barrier semaphores. Data moves between devices by JAX's collectives and lax.ppermute only.
A program may use at most 64 MiB of HBM per device.

v0:
```python
import jax
import jax.numpy as jnp
from jax import lax
from jax.sharding import Mesh
from jax.sharding import PartitionSpec as P

EP = ("ep_0", "ep_1")
REP_EP = ("rep", "ep_0", "ep_1")


def cut_along(value, dim, size):
    before, after = (value.shape[:dim], value.shape[dim + 1 :])
    return jnp.moveaxis(value.reshape(*before, size, -1, *after), dim, 0)


def laid_out(blocks, dim):
    blocks = jnp.moveaxis(blocks, 0, dim)
    shape = blocks.shape
    return blocks.reshape(*shape[:dim], shape[dim] * shape[dim + 1], *shape[dim + 2 :])


def moved_by_axis(blocks, axes, sequence):
    inside = blocks.shape[1:]
    whole = blocks.reshape(*(lax.axis_size(a) for a in axes), *inside)
    for k in sequence:
        whole = lax.all_to_all(whole, axes[k], k, k, tiled=True)
    return whole.reshape(-1, *inside)


def exchange_by_chip(value, groups, sequence, split_dim, concat_dim):
    size = lax.axis_size(groups[0]) * lax.axis_size(groups[1])
    blocks = cut_along(value, split_dim, size)
    return laid_out(moved_by_axis(blocks, groups, sequence), concat_dim)


def slot_tables(routing, route_gates, experts, capacity):
    count_rows = routing.shape[0]
    choices_n = routing.shape[1]
    flat_ids = routing.reshape(-1)
    onehot = (flat_ids[:, None] == jnp.arange(experts, dtype=jnp.int32)[None, :]).astype(jnp.int32)
    before = jnp.cumsum(onehot, axis=0) - onehot
    position = jnp.sum(before * onehot, axis=1)
    slot_index = flat_ids * capacity + position
    picked = (
        slot_index[:, None] == jnp.arange(experts * capacity, dtype=jnp.int32)[None, :]
    ).astype(jnp.float32)
    dispatch = picked.reshape(count_rows, choices_n, experts * capacity).sum(axis=1)
    combine = (
        (picked * route_gates.reshape(-1)[:, None])
        .reshape(count_rows, choices_n, experts * capacity)
        .sum(axis=1)
    )
    return (dispatch, combine)


def hidden_rows(everyone, expert_gate, expert_up, capacity):
    local_count = expert_gate.shape[0]
    total = everyone.shape[0]
    row_block = everyone.reshape(
        total // (local_count * capacity), local_count, capacity, everyone.shape[1]
    )
    gate_part = jnp.einsum(
        "tlcd,ldf->tlcf", row_block, expert_gate, preferred_element_type=jnp.float32
    )
    upward = jnp.einsum("tlcd,ldf->tlcf", row_block, expert_up, preferred_element_type=jnp.float32)
    return (jax.nn.silu(gate_part) * upward).astype(jnp.bfloat16)


def body(tokens, routing, route_gates, expert_gate, expert_up, expert_down):
    local_count = expert_gate.shape[0]
    ep_count = lax.axis_size(EP)
    tp_count = lax.axis_size("tp")
    tok_count = tokens.shape[0]
    capacity = 2 * tok_count // ep_count + tok_count // 16
    experts = local_count * ep_count
    dispatch, combine = slot_tables(routing, route_gates, experts, capacity)
    dispatch_low = dispatch.astype(jnp.bfloat16)
    whole = lax.all_gather(tokens, "tp", axis=1, tiled=True)
    packed = jnp.einsum(
        "tc,td->cd", dispatch_low, whole, preferred_element_type=jnp.float32
    ).astype(jnp.bfloat16)
    everyone = exchange_by_chip(packed, ("ep_0", "ep_1"), (0, 1), 0, 0)
    total_rows = everyone.shape[0]
    columns = everyone.shape[1]
    hidden = hidden_rows(everyone, expert_gate, expert_up, capacity)
    part = jnp.einsum("tlcf,lfd->dtlc", hidden, expert_down, preferred_element_type=jnp.float32)
    summed_t = lax.psum_scatter(
        part.reshape(columns // tp_count * lax.axis_size("tp"), total_rows),
        "tp",
        scatter_dimension=0,
        tiled=True,
    )
    summed = summed_t.T
    expert_out = summed.astype(jnp.bfloat16)
    returned = lax.all_to_all(expert_out, EP, split_axis=0, concat_axis=0, tiled=True)
    mixed = jnp.dot(combine, returned.astype(jnp.float32))
    return mixed.astype(jnp.bfloat16)


def solution(mesh):
    finer = Mesh(
        mesh.devices.reshape(mesh.shape["rep"], mesh.shape["tp"], 4, 2),
        ("rep", "tp", "ep_0", "ep_1"),
    )
    placed = (
        P(REP_EP, "tp"),
        P(REP_EP, None),
        P(REP_EP, None),
        P(EP, None, "tp"),
        P(EP, None, "tp"),
        P(EP, "tp", None),
    )
    return jax.shard_map(
        body, mesh=finer, in_specs=placed, out_specs=P(REP_EP, "tp"), check_vma=False
    )
```

profile of v0, /device:TPU:38, one launch (start us, length us, event | category | flops | bytes accessed | tf_op | source)
XLA Modules:
  0.0 285.1 jit_solution(12481308610090394626)
XLA Ops:
  6.5 0.0 copy-start
  6.6 0.0 reduce-scatter.4.cloned.1.call-start
  6.6 0.9 copy.31
  7.5 0.8 copy.29
  8.3 0.1 eq.37
  8.5 0.6 reduce-window.6
  9.0 0.2 slice_reduce_fusion
  9.3 0.1 add_bitcast_fusion
  9.4 0.1 reduce_sum.30
  9.5 0.1 copy.30
  9.6 0.7 multiply_add_fusion
  10.3 99.1 %all_gather.3 = bf16[96,3072]{0,1:T(8,128)(2,1)S(1)} all-gather(bf16[96,96]{0,1:T(8,128)(2,1)S(1)} %copy.31), channel_id=1, replica_groups=mesh['rep'=2,'tp'=32,'ep_0'=4,'ep_1'=2] {'tp'}, dimensions={1}, use_global_device_ids=true | all-gather | bytes 608256 | tf_op jit(solution)/shard_map/all_gather | solution.py:78
  109.4 0.8 convert_reduce_fusion
  110.3 1.7 convolution_convert_fusion
  112.0 1.6 reshape_reshape.3
  113.5 1.5 copy.32
  115.1 15.6 %all_to_all.22 = bf16[4,2,30,3072]{3,1,2,0:T(2,128)(2,1)S(1)} all-to-all(bf16[4,2,30,3072]{3,1,2,0:T(2,128)(2,1)S(1)} %copy.32), channel_id=1, replica_groups=mesh['rep'=2,'tp'=32,'ep_0'=4,'ep_1'=2] {'ep_0'}, dimensions={0} | all-to-all | bytes 2949120 | tf_op jit(solution)/shard_map/all_to_all | solution.py:26
  130.6 0.8 copy.33
  131.4 4.9 %all_to_all.23 = bf16[4,2,30,3072]{3,0,2,1:T(4,128)(2,1)S(1)} all-to-all(bf16[4,2,30,3072]{3,0,2,1:T(4,128)(2,1)S(1)} %copy.33), channel_id=1, replica_groups=mesh['rep'=2,'tp'=32,'ep_0'=4,'ep_1'=2] {'ep_1'}, dimensions={1} | all-to-all | bytes 2949120 | tf_op jit(solution)/shard_map/all_to_all | solution.py:26
  136.3 0.0 copy-start.1
  136.3 0.5 copy.34
  136.8 0.9 copy-done.1
  137.7 0.0 copy-start.2
  137.7 0.6 fusion.5
  138.3 0.8 copy-done.2
  139.1 0.6 fusion.14
  139.8 0.0 copy-done
  139.8 2.2 convolution_bitcast_fusion
  141.9 3.5 %copy.35 = f32[3072,240]{1,0:T(8,128)} copy(f32[3072,240]{0,1:T(8,128)} %convolution_bitcast_fusion) | data formatting | bytes 5898240
  145.5 0.1 reduce-scatter.4.cloned.1.call-update
  145.5 122.7 %reduce-scatter.4.cloned.1.call-done = f32[96,240]{1,0:T(8,128)} async-done(((f32[3072,240]{1,0:T(8,128)}), f32[96,240]{1,0:T(8,128)}) %reduce-scatter.4.cloned.1.call-update) | async-done | bytes 92176
  268.2 1.0 copy.36
  269.2 8.2 %all_to_all.24 = bf16[8,30,96]{2,1,0:T(8,128)(2,1)S(1)} all-to-all(bf16[8,30,96]{2,1,0:T(8,128)(2,1)S(1)} %all_to_all.16), channel_id=1, replica_groups=mesh['rep'=2,'tp'=32,'ep_0'=4,'ep_1'=2] {'ep_0','ep_1'}, dimensions={0} | all-to-all | bytes 92160 | tf_op jit(solution)/shard_map/all_to_all | solution.py:95
  277.4 0.8 fusion.20
  (8 shorter events, 0.2 us)
Async XLA Ops:
  6.5 133.2 %copy-start = (bf16[1,256,3072]{2,1,0:T(8,128)(2,1)S(1)}, bf16[1,256,3072]{2,1,0:T(8,128)(2,1)}, u32[]{:S(2)}) copy-start(bf16[1,256,3072]{2,1,0:T(8,128)(2,1)} %param.11) | copy-start | bytes 4718596
  6.6 261.7 %reduce-scatter.4.cloned.1.call-start = ((), (), s32[]{:S(2)}) async-start(), calls=%async_computation.4 | async-start | bytes 3244032
  136.3 1.4 copy-start.1
  137.7 1.4 copy-start.2
Sparse Core Ops, SparseCore 0:
  145.6 122.5 reduce-scatter.3
where the time goes:
time: 288 us; the launch traced here: 285 us
  blocking collectives  128 us (44%)
  waiting for transfers between devices  123 us (43%)
  between operations  13.5 us (5%)
  local copies, waits for them, and re-layouts  13 us (5%)
  matrix products  5.83 us (2%)
    unnamed x2, waiting for transfers between devices  123 us
    all_gather x1, blocking collectives, body(): whole = lax.all_gather(tokens, 'tp', axis=1, tiled=True)  99.1 us
    all_to_all x2, blocking collectives, moved_by_axis(): whole = lax.all_to_all(whole, axes[k], k, k, tiled=True)  20.5 us
    all_to_all x1, blocking collectives, body(): lax.all_to_all(expert_out, EP, split_axis=0, concat_axis=0, tiled=True)  8.16 us
    unnamed x10, local copies, waits for them, and re-layouts  8.02 us
  transfers between devices with their start and end apart: 1, of which 1 were waited for; matrix products, arithmetic and copies ran while one was open for 0% of the time, Pallas kernels for 0%

commit v1 on v0

v1 whole, which is shorter than its diff:
```python
import jax
import jax.numpy as jnp
from jax import lax
from jax.sharding import Mesh
from jax.sharding import PartitionSpec as P

REP_EP = ("rep", "ep")
TP = ("hi", "lo")
BF = jnp.bfloat16
F32 = jnp.float32
LO = 2


def slot_tables(routing, route_gates, experts, rows):
    tok_count, choices_n = routing.shape
    flat_ids = routing.reshape(-1)
    onehot = (flat_ids[:, None] == jnp.arange(experts, dtype=jnp.int32)[None, :]).astype(BF)
    n = tok_count * choices_n
    earlier = (jnp.arange(n)[None, :] < jnp.arange(n)[:, None]).astype(BF)
    before = jnp.dot(earlier, onehot, preferred_element_type=F32)
    position = jnp.sum(before * onehot.astype(F32), axis=1).astype(jnp.int32)
    slot = (flat_ids * rows + position).reshape(tok_count, choices_n)
    picked = slot[:, :, None] == jnp.arange(experts * rows, dtype=jnp.int32)[None, None, :]
    dispatch = picked.astype(F32).sum(axis=1).astype(BF)
    combine = jnp.where(picked, route_gates[:, :, None], 0.0).sum(axis=1)
    return dispatch, combine


def body(tokens, routing, route_gates, expert_gate, expert_up, expert_down):
    ep_count = lax.axis_size("ep")
    hi_count = lax.axis_size("hi")
    tok_count, feat = tokens.shape
    capacity = 2 * tok_count // ep_count + tok_count // 16
    rows = -(-capacity // 8) * 8
    slots = ep_count * rows
    wide = hi_count * feat
    hidden_n = expert_gate.shape[2]

    own = jnp.broadcast_to(tokens.T[None], (hi_count, feat, tok_count))
    gathered = lax.all_to_all(own, "hi", 0, 0, tiled=True).reshape(wide, tok_count)
    dispatch, combine = slot_tables(routing, route_gates, ep_count, rows)
    packed = lax.dot_general(
        dispatch, gathered, (((0,), (1,)), ((), ())), preferred_element_type=F32
    ).astype(BF)
    sent = jnp.broadcast_to(packed.reshape(1, ep_count, rows, wide), (LO, ep_count, rows, wide))
    got = lax.all_to_all(
        sent.reshape(LO * ep_count, rows, wide), ("lo", "ep"), 0, 0, tiled=True
    ).reshape(LO, slots, wide)

    def by_lo(w):
        return w.reshape(hi_count, LO, feat, hidden_n).transpose(1, 0, 2, 3).reshape(LO, wide, hidden_n)

    w_gate, w_up = by_lo(expert_gate), by_lo(expert_up)
    gate = sum(jnp.dot(got[i], w_gate[i], preferred_element_type=F32) for i in range(LO))
    up = sum(jnp.dot(got[i], w_up[i], preferred_element_type=F32) for i in range(LO))
    hidden = (jax.nn.silu(gate) * up).astype(BF)

    w_down = (
        expert_down.reshape(hidden_n, hi_count, LO, feat)
        .transpose(2, 0, 1, 3)
        .reshape(LO, hidden_n, wide)
    )
    part = jnp.stack([jnp.dot(hidden, w_down[i], preferred_element_type=F32).astype(BF) for i in range(LO)])
    back = lax.all_to_all(
        part.reshape(LO * ep_count, rows, wide), ("lo", "ep"), 0, 0, tiled=True
    ).reshape(LO * slots, wide)
    weights = jnp.concatenate([combine] * LO, axis=1).astype(BF)
    mixed = lax.dot_general(
        back, weights, (((0,), (1,)), ((), ())), preferred_element_type=F32
    ).astype(BF)
    shares = lax.all_to_all(
        mixed.reshape(hi_count, feat, tok_count), "hi", 0, 0, tiled=True
    )
    return jnp.sum(shares.astype(F32), axis=0).astype(BF).T


def solution(mesh):
    finer = Mesh(
        mesh.devices.reshape(
            mesh.shape["rep"], mesh.shape["tp"] // LO, LO, mesh.shape["ep"]
        ),
        ("rep", "hi", "lo", "ep"),
    )
    placed = (
        P(REP_EP, TP),
        P(REP_EP, None),
        P(REP_EP, None),
        P("ep", None, TP),
        P("ep", None, TP),
        P("ep", TP, None),
    )
    return jax.shard_map(
        body, mesh=finer, in_specs=placed, out_specs=P(REP_EP, TP), check_vma=False
    )
```

time: 288 us -> 210 us (0.73)
  waiting for transfers between devices: 123 us -> 45.2 us
  starting transfers between devices: 0.01 us -> 61.8 us
  blocking collectives: 128 us -> 81.1 us
  between operations: 13.5 us -> 0.19 us
    unnamed x2 -> x0, waiting for transfers between devices: 123 us -> none
    all_gather x1 -> x0, blocking collectives: 99.1 us -> none  [body(): whole = lax.all_gather(tokens, 'tp', axis=1, tiled=True)]
    all_to_all x0 -> x2, starting transfers between devices: none -> 61.8 us  [the longest x1 44.6 us: body(): lax.all_to_all(own, 'hi', 0, 0, tiled=True).reshape(wide, tok_count)]
    all_to_all x3 -> x2, blocking collectives: 28.6 us -> 81.1 us  [the longest x1 56.9 us: body(): lax.all_to_all(mixed.reshape(hi_count, feat, tok_count), 'hi', 0, 0, tile...]
    all_to_all x0 -> x2, waiting for transfers between devices: none -> 45.2 us  [the longest x1 30.8 us: body(): lax.all_to_all(own, 'hi', 0, 0, tiled=True).reshape(wide, tok_count)]
    slice x1 -> x4, local copies, waits for them, and re-layouts: 0.21 us -> 5.42 us  [the longest x1 2.74 us: body(): w_gate[i]]
    unnamed x10 -> x16, local copies, waits for them, and re-layouts: 8.02 us -> 4.42 us
    another operation x3 -> x0, local copies, waits for them, and re-layouts: 3.08 us -> none  [the longest x2 3.07 us: moved_by_axis(): whole = blocks.reshape(*(lax.axis_size(a) for a in axes), *inside)]
  transfers between devices with their start and end apart: 1 -> 2, of which waited for: 1 -> 2; matrix products, arithmetic and copies ran while one was open for 0% -> 5% of each run, Pallas kernels for 0% -> 0%
where the time goes in v1:
time: 210 us; the launch traced here: 207 us
  blocking collectives  81.1 us (39%)
  starting transfers between devices  61.8 us (29%)
  waiting for transfers between devices  45.2 us (22%)
  local copies, waits for them, and re-layouts  13.6 us (6%)
  matrix products  3.21 us (2%)
  other arithmetic  2.36 us (1%)
    all_to_all x1, blocking collectives, body(): lax.all_to_all(mixed.reshape(hi_count, feat, tok_count), 'hi', 0, 0, tile...  56.9 us
    all_to_all x1, starting transfers between devices, body(): lax.all_to_all(own, 'hi', 0, 0, tiled=True).reshape(wide, tok_count)  44.6 us
    all_to_all x1, waiting for transfers between devices, body(): lax.all_to_all(own, 'hi', 0, 0, tiled=True).reshape(wide, tok_count)  30.8 us
    all_to_all x1, blocking collectives, body(): lax.all_to_all(part.reshape(LO * ep_count, rows, wide), ('lo', 'ep'), 0,...  24.2 us
    all_to_all x1, starting transfers between devices, body(): lax.all_to_all(sent.reshape(LO * ep_count, rows, wide), ('lo', 'ep'), 0,...  17.2 us
    all_to_all x1, waiting for transfers between devices, body(): lax.all_to_all(sent.reshape(LO * ep_count, rows, wide), ('lo', 'ep'), 0,...  14.4 us
    unnamed x16, local copies, waits for them, and re-layouts  4.42 us
  transfers between devices with their start and end apart: 2, of which 2 were waited for; matrix products, arithmetic and copies ran while one was open for 5% of the time, Pallas kernels for 0%

profile of v1, /device:TPU:38, one launch (start us, length us, event | category | flops | bytes accessed | tf_op | source)
XLA Modules:
  0.0 207.5 jit_solution(2862732457851859951)
XLA Ops:
  0.0 0.8 copy.32
  0.8 0.8 broadcast_in_dim.18
  1.6 44.6 %all-to-all-start = ((bf16[16,96,96]{2,1,0:T(8,128)(2,1)}), bf16[16,96,96]{2,1,0:T(8,128)(2,1)S(1)}, u32[]{:S(2)}, u32[]{:S(2)}) async-start(bf16[16,96,96]{2,1,0:T(8,128)(2,1)} %broadcast_in_dim.18), calls=%async_computation | async-start | bytes 786432 | tf_op jit(solution)/shard_map/all_to_all | solution.py:40
  46.2 0.8 copy.30
  47.0 0.1 eq.28
  47.1 0.2 fusion.4
  47.3 0.1 convert_element_type.42
  47.5 0.1 copy.31
  47.6 0.7 multiply_add_fusion
  48.3 0.8 select_reduce_fusion
  49.1 30.8 %all-to-all-done = bf16[16,96,96]{2,1,0:T(8,128)(2,1)S(1)} async-done(((bf16[16,96,96]{2,1,0:T(8,128)(2,1)}), bf16[16,96,96]{2,1,0:T(8,128)(2,1)S(1)}, u32[]{:S(2)}, u32[]{:S(2)}) %all-to-all-start) | async-done | bytes 294944 | tf_op jit(solution)/shard_map/all_to_all | solution.py:40
  79.9 0.4 convolution_convert_fusion.2
  80.3 1.3 broadcast_in_dim.32
  81.6 17.2 %all-to-all-start.1 = ((bf16[16,32,1536]{2,1,0:T(8,128)(2,1)}), bf16[16,32,1536]{2,1,0:T(8,128)(2,1)S(1)}, u32[]{:S(2)}, u32[]{:S(2)}) async-start(bf16[16,32,1536]{2,1,0:T(8,128)(2,1)} %bitcast.3), calls=%async_computation.1 | async-start | bytes 3145728 | tf_op jit(solution)/shard_map/all_to_all | solution.py:46
  98.8 1.7 copy.33
  100.6 0.0 copy-start.5
  100.6 2.7 %fusion.13 = (bf16[1,16,96,256]{3,2,0,1:T(8,128)(2,1)}, bf16[1,16,96,256]{3,2,0,1:T(8,128)(2,1)}) fusion(bf16[2,16,96,256]{3,2,0,1:T(8,128)(2,1)} %bitcast.58), kind=kLoop, calls=%fused_computation.27 | loop fusion | bytes 3145728 | tf_op jit(solution)/shard_map/slice | solution.py:54
  103.3 0.0 copy-done.5
  103.3 1.3 fusion.14
  104.6 1.3 fusion.12
  105.9 0.0 copy-start
  105.9 14.4 %all-to-all-done.1 = bf16[16,32,1536]{2,1,0:T(8,128)(2,1)S(1)} async-done(((bf16[16,32,1536]{2,1,0:T(8,128)(2,1)}), bf16[16,32,1536]{2,1,0:T(8,128)(2,1)S(1)}, u32[]{:S(2)}, u32[]{:S(2)}) %all-to-all-start.1) | async-done | bytes 1572896 | tf_op jit(solution)/shard_map/all_to_all | solution.py:46
  120.3 0.1 fusion.15
  120.4 0.0 copy-start.1
  120.4 0.0 copy-done
  120.4 0.0 copy-start.4
  120.4 0.4 fusion.16
  120.8 0.7 copy-done.1
  121.5 0.0 copy-start.6
  121.5 0.4 fusion.17
  121.9 0.0 copy-done.4
  121.9 0.4 convolution_add_fusion.1
  122.3 0.0 copy-start.3
  122.3 0.4 copy-done.6
  122.7 0.4 fusion.3
  123.1 0.0 copy-start.2
  123.1 0.4 copy-done.3
  123.5 0.4 fusion
  123.9 0.4 copy-done.2
  124.3 0.4 fusion.1
  124.7 0.1 pad_maximum_fusion
  124.8 24.2 %all_to_all.20 = bf16[16,32,1536]{2,1,0:T(8,128)(2,1)S(1)} all-to-all(bf16[16,32,1536]{2,1,0:T(8,128)(2,1)S(1)} %bitcast.48), channel_id=1, replica_groups=mesh['rep'=2,'hi'=16,'lo'=2,'ep'=8] {'lo','ep'}, dimensions={0} | all-to-all | bytes 3145728 | tf_op jit(solution)/shard_map/all_to_all | solution.py:64
  149.1 0.4 convolution_convert_fusion.3
  149.5 0.3 reshape.65
  149.8 0.1 copy.34
  149.9 56.9 %all_to_all.21 = bf16[16,96,96]{1,2,0:T(8,128)(2,1)S(1)} all-to-all(bf16[16,96,96]{1,2,0:T(8,128)(2,1)S(1)} %copy.34), channel_id=1, replica_groups=mesh['rep'=2,'hi'=16,'lo'=2,'ep'=8] {'hi'}, dimensions={0} | all-to-all | bytes 589824 | tf_op jit(solution)/shard_map/all_to_all | solution.py:71
  206.8 0.7 reduce_sum.42
  (1 shorter events, 0.0 us)
Async XLA Ops:
  1.6 78.2 %all-to-all-start = ((bf16[16,96,96]{2,1,0:T(8,128)(2,1)}), bf16[16,96,96]{2,1,0:T(8,128)(2,1)S(1)}, u32[]{:S(2)}, u32[]{:S(2)}) async-start(bf16[16,96,96]{2,1,0:T(8,128)(2,1)} %broadcast_in_dim.18), calls=%async_computation | async-start | bytes 786432 | tf_op jit(solution)/shard_map/all_to_all | solution.py:40
  81.6 38.7 %all-to-all-start.1 = ((bf16[16,32,1536]{2,1,0:T(8,128)(2,1)}), bf16[16,32,1536]{2,1,0:T(8,128)(2,1)S(1)}, u32[]{:S(2)}, u32[]{:S(2)}) async-start(bf16[16,32,1536]{2,1,0:T(8,128)(2,1)} %bitcast.3), calls=%async_computation.1 | async-start | bytes 3145728 | tf_op jit(solution)/shard_map/all_to_all | solution.py:46
  100.6 2.8 %copy-start.5 = (bf16[1,3072,256]{2,1,0:T(8,128)(2,1)S(1)}, bf16[1,3072,256]{2,1,0:T(8,128)(2,1)}, u32[]{:S(2)}) copy-start(bf16[1,3072,256]{2,1,0:T(8,128)(2,1)} %param.10) | copy-start | bytes 4718596
  105.9 14.5 %copy-start = (bf16[1,16,96,256]{3,2,0,1:T(8,128)(2,1)S(1)}, bf16[1,16,96,256]{3,2,0,1:T(8,128)(2,1)}, u32[]{:S(2)}) copy-start(bf16[1,16,96,256]{3,2,0,1:T(8,128)(2,1)} %get-tuple-element.10) | copy-start | bytes 2359300
  120.4 1.1 copy-start.1
  120.4 1.5 copy-start.4
  121.5 1.2 copy-start.6
  122.3 1.2 copy-start.3
  123.1 1.2 copy-start.2

commit v2 on v1

--- a/solution.py
+++ b/solution.py
@@ -36,8 +36,7 @@
     wide = hi_count * feat
     hidden_n = expert_gate.shape[2]
 
-    own = jnp.broadcast_to(tokens.T[None], (hi_count, feat, tok_count))
-    gathered = lax.all_to_all(own, "hi", 0, 0, tiled=True).reshape(wide, tok_count)
+    gathered = lax.all_gather(tokens.T, "hi", axis=0, tiled=True)
     dispatch, combine = slot_tables(routing, route_gates, ep_count, rows)
     packed = lax.dot_general(
         dispatch, gathered, (((0,), (1,)), ((), ())), preferred_element_type=F32

time: 210 us -> 196 us (0.933)
  blocking collectives: 81.1 us -> 155 us
  starting transfers between devices: 61.8 us -> 5.83 us
  waiting for transfers between devices: 45.2 us -> 14.4 us
    all_gather x0 -> x1, blocking collectives: none -> 75 us  [body(): gathered = lax.all_gather(tokens.T, 'hi', axis=0, tiled=True)]
    all_to_all x1 -> x0, starting transfers between devices: 44.6 us -> none  [body(): lax.all_to_all(own, 'hi', 0, 0, tiled=True).reshape(wide, tok_count)]
    all_to_all x1 -> x0, waiting for transfers between devices: 30.8 us -> none  [body(): lax.all_to_all(own, 'hi', 0, 0, tiled=True).reshape(wide, tok_count)]
    all_to_all x1, starting transfers between devices: 17.2 us -> 5.83 us  [body(): lax.all_to_all(sent.reshape(LO * ep_count, rows, wide), ('lo', 'ep'), 0,...]
    unnamed x16 -> x17, local copies, waits for them, and re-layouts: 4.42 us -> 5.24 us
  transfers between devices with their start and end apart: 2 -> 1, of which waited for: 2 -> 1; matrix products, arithmetic and copies ran while one was open for 5% -> 4% of each run, Pallas kernels for 0% -> 0%
where the time goes in v2:
time: 196 us; the launch traced here: 194 us
  blocking collectives  155 us (79%)
  waiting for transfers between devices  14.4 us (7%)
  local copies, waits for them, and re-layouts  12.8 us (7%)
  starting transfers between devices  5.83 us (3%)
  matrix products  3.23 us (2%)
  other arithmetic  2.36 us (1%)
    all_gather x1, blocking collectives, body(): gathered = lax.all_gather(tokens.T, 'hi', axis=0, tiled=True)  75 us
    all_to_all x1, blocking collectives, body(): lax.all_to_all(mixed.reshape(hi_count, feat, tok_count), 'hi', 0, 0, tile...  55.6 us
    all_to_all x1, blocking collectives, body(): lax.all_to_all(part.reshape(LO * ep_count, rows, wide), ('lo', 'ep'), 0,...  24.2 us
    all_to_all x1, waiting for transfers between devices, body(): lax.all_to_all(sent.reshape(LO * ep_count, rows, wide), ('lo', 'ep'), 0,...  14.4 us
    all_to_all x1, starting transfers between devices, body(): lax.all_to_all(sent.reshape(LO * ep_count, rows, wide), ('lo', 'ep'), 0,...  5.83 us
    unnamed x17, local copies, waits for them, and re-layouts  5.24 us
  transfers between devices with their start and end apart: 1, of which 1 were waited for; matrix products, arithmetic and copies ran while one was open for 4% of the time, Pallas kernels for 0%

profile of v2, /device:TPU:38, one launch (start us, length us, event | category | flops | bytes accessed | tf_op | source)
XLA Modules:
  0.0 193.6 jit_solution(637232276068174422)
XLA Ops:
  0.0 0.8 copy.28
  0.8 0.1 eq.28
  0.9 0.2 fusion.4
  1.1 0.1 convert_element_type.42
  1.2 0.1 copy.29
  1.3 0.7 multiply_add_fusion
  2.0 0.8 copy.30
  2.9 75.0 %all_gather.3 = bf16[1536,96]{1,0:T(8,128)(2,1)S(1)} all-gather(bf16[96,96]{1,0:T(8,128)(2,1)S(1)} %bitcast.60), channel_id=1, replica_groups=mesh['rep'=2,'hi'=16,'lo'=2,'ep'=8] {'hi'}, dimensions={0}, use_global_device_ids=true | all-gather | bytes 313344 | tf_op jit(solution)/shard_map/all_gather | solution.py:39
  77.8 0.8 select_reduce_fusion
  78.6 0.4 convolution_convert_fusion.2
  79.0 1.3 broadcast_in_dim.25
  80.4 5.8 %all-to-all-start = ((bf16[16,32,1536]{2,1,0:T(8,128)(2,1)}), bf16[16,32,1536]{2,1,0:T(8,128)(2,1)S(1)}, u32[]{:S(2)}, u32[]{:S(2)}) async-start(bf16[16,32,1536]{2,1,0:T(8,128)(2,1)} %bitcast.2), calls=%async_computation | async-start | bytes 3145728 | tf_op jit(solution)/shard_map/all_to_all | solution.py:45
  86.2 1.7 copy.31
  87.9 0.0 copy-start.5
  87.9 2.7 %fusion.13 = (bf16[1,16,96,256]{3,2,0,1:T(8,128)(2,1)}, bf16[1,16,96,256]{3,2,0,1:T(8,128)(2,1)}) fusion(bf16[2,16,96,256]{3,2,0,1:T(8,128)(2,1)} %bitcast.57), kind=kLoop, calls=%fused_computation.27 | loop fusion | bytes 3145728 | tf_op jit(solution)/shard_map/slice | solution.py:53
  90.7 0.0 copy-done.5
  90.7 1.3 fusion.14
  92.0 1.3 fusion.12
  93.3 0.0 copy-start
  93.3 14.4 %all-to-all-done = bf16[16,32,1536]{2,1,0:T(8,128)(2,1)S(1)} async-done(((bf16[16,32,1536]{2,1,0:T(8,128)(2,1)}), bf16[16,32,1536]{2,1,0:T(8,128)(2,1)S(1)}, u32[]{:S(2)}, u32[]{:S(2)}) %all-to-all-start) | async-done | bytes 1572896 | tf_op jit(solution)/shard_map/all_to_all | solution.py:45
  107.6 0.1 fusion.15
  107.7 0.0 copy-start.1
  107.7 0.0 copy-done
  107.7 0.0 copy-start.4
  107.8 0.4 fusion.16
  108.1 0.7 copy-done.1
  108.9 0.0 copy-start.6
  108.9 0.4 fusion.17
  109.2 0.0 copy-done.4
  109.2 0.4 convolution_add_fusion.1
  109.6 0.0 copy-start.3
  109.6 0.4 copy-done.6
  110.1 0.4 fusion.3
  110.4 0.0 copy-start.2
  110.4 0.4 copy-done.3
  110.8 0.4 fusion
  111.2 0.4 copy-done.2
  111.6 0.4 fusion.1
  112.0 0.1 pad_maximum_fusion
  112.2 24.2 %all_to_all.15 = bf16[16,32,1536]{2,1,0:T(8,128)(2,1)S(1)} all-to-all(bf16[16,32,1536]{2,1,0:T(8,128)(2,1)S(1)} %bitcast.47), channel_id=1, replica_groups=mesh['rep'=2,'hi'=16,'lo'=2,'ep'=8] {'lo','ep'}, dimensions={0} | all-to-all | bytes 3145728 | tf_op jit(solution)/shard_map/all_to_all | solution.py:63
  136.4 0.4 convolution_convert_fusion.3
  136.8 0.3 reshape.60
  137.2 0.1 copy.32
  137.3 55.6 %all_to_all.16 = bf16[16,96,96]{1,2,0:T(8,128)(2,1)S(1)} all-to-all(bf16[16,96,96]{1,2,0:T(8,128)(2,1)S(1)} %copy.32), channel_id=1, replica_groups=mesh['rep'=2,'hi'=16,'lo'=2,'ep'=8] {'hi'}, dimensions={0} | all-to-all | bytes 589824 | tf_op jit(solution)/shard_map/all_to_all | solution.py:70
  192.9 0.7 reduce_sum.42
  (1 shorter events, 0.0 us)
Async XLA Ops:
  80.4 27.3 %all-to-all-start = ((bf16[16,32,1536]{2,1,0:T(8,128)(2,1)}), bf16[16,32,1536]{2,1,0:T(8,128)(2,1)S(1)}, u32[]{:S(2)}, u32[]{:S(2)}) async-start(bf16[16,32,1536]{2,1,0:T(8,128)(2,1)} %bitcast.2), calls=%async_computation | async-start | bytes 3145728 | tf_op jit(solution)/shard_map/all_to_all | solution.py:45
  87.9 2.8 %copy-start.5 = (bf16[1,3072,256]{2,1,0:T(8,128)(2,1)S(1)}, bf16[1,3072,256]{2,1,0:T(8,128)(2,1)}, u32[]{:S(2)}) copy-start(bf16[1,3072,256]{2,1,0:T(8,128)(2,1)} %param.10) | copy-start | bytes 4718596
  93.3 14.5 %copy-start = (bf16[1,16,96,256]{3,2,0,1:T(8,128)(2,1)S(1)}, bf16[1,16,96,256]{3,2,0,1:T(8,128)(2,1)}, u32[]{:S(2)}) copy-start(bf16[1,16,96,256]{3,2,0,1:T(8,128)(2,1)} %get-tuple-element.10) | copy-start | bytes 2359300
  107.7 1.1 copy-start.1
  107.7 1.5 copy-start.4
  108.9 1.2 copy-start.6
  109.6 1.2 copy-start.3
  110.4 1.2 copy-start.2

commit v3 on v2

v3 whole, which is shorter than its diff:
```python
import functools

import jax
import jax.numpy as jnp
from jax import lax
from jax.experimental import pallas as pl
from jax.experimental.pallas import tpu as pltpu
from jax.sharding import Mesh
from jax.sharding import PartitionSpec as P

REP_EP = ("rep", "ep")
TP = ("hi", "lo")
BF = jnp.bfloat16
F32 = jnp.float32
LO = 2


def held_close(value):
    return pltpu.with_memory_space_constraint(value, pltpu.VMEM)


def slot_match(routing_ref, experts, rows):
    tok_count = routing_ref.shape[1]
    shape = (experts * rows, tok_count)
    slot = lax.broadcasted_iota(jnp.int32, shape, 0)
    expert, place = slot // rows, slot % rows
    named = (routing_ref[0:1, :] == expert) | (routing_ref[1:2, :] == expert)
    square = (tok_count, tok_count)
    earlier = lax.broadcasted_iota(jnp.int32, square, 0) < lax.broadcasted_iota(jnp.int32, square, 1)
    before = jnp.dot(
        named.astype(F32).astype(BF), earlier.astype(F32).astype(BF), preferred_element_type=F32
    )
    return expert, named & (before == place.astype(F32))


def pack_kernel(experts, rows, routing_ref, tokens_ref, out_ref, whole_ref):
    hi_count, _, feat = tokens_ref.shape
    _, held = slot_match(routing_ref, experts, rows)
    dispatch = held.astype(F32).astype(BF)
    for i in range(hi_count):
        whole_ref[:, i * feat : (i + 1) * feat] = tokens_ref[i]
    packed = jnp.dot(dispatch, whole_ref[...], preferred_element_type=F32).astype(BF)
    for i in range(out_ref.shape[0]):
        out_ref[i] = packed


def combine_kernel(experts, rows, routing_ref, gates_ref, back_ref, out_ref):
    hi_count, _, feat = out_ref.shape
    expert, held = slot_match(routing_ref, experts, rows)
    weight = jnp.where(routing_ref[0:1, :] == expert, gates_ref[0:1, :], gates_ref[1:2, :])
    weight = jnp.where(held, weight, 0.0).astype(BF)
    weight = jnp.concatenate([weight] * LO, axis=0)
    mixed = lax.dot_general(
        weight, back_ref[...], (((0,), (0,)), ((), ())), preferred_element_type=F32
    ).astype(BF)
    for i in range(hi_count):
        out_ref[i] = mixed[:, i * feat : (i + 1) * feat]


def body(tokens, routing, route_gates, expert_gate, expert_up, expert_down):
    ep_count = lax.axis_size("ep")
    hi_count = lax.axis_size("hi")
    tok_count, feat = tokens.shape
    capacity = 2 * tok_count // ep_count + tok_count // 16
    rows = -(-capacity // 16) * 16
    slots = ep_count * rows
    wide = hi_count * feat
    hidden_n = expert_gate.shape[2]
    in_vmem = pl.BlockSpec(memory_space=pltpu.VMEM)

    gathered = lax.all_gather(tokens, "hi", axis=0)
    sent = pl.pallas_call(
        functools.partial(pack_kernel, ep_count, rows),
        out_shape=pltpu.VMEM((LO, slots, wide), BF),
        in_specs=[in_vmem, in_vmem],
        out_specs=in_vmem,
        scratch_shapes=[pltpu.VMEM((tok_count, wide), BF)],
        name="pack",
    )(routing.T, held_close(gathered))
    got = lax.all_to_all(
        sent.reshape(LO * ep_count, rows, wide), ("lo", "ep"), 0, 0, tiled=True
    ).reshape(LO, slots, wide)

    def by_lo(w):
        return w.reshape(hi_count, LO, feat, hidden_n).transpose(1, 0, 2, 3).reshape(LO, wide, hidden_n)

    w_gate, w_up = by_lo(expert_gate), by_lo(expert_up)
    gate = sum(jnp.dot(got[i], w_gate[i], preferred_element_type=F32) for i in range(LO))
    up = sum(jnp.dot(got[i], w_up[i], preferred_element_type=F32) for i in range(LO))
    hidden = (jax.nn.silu(gate) * up).astype(BF)

    w_down = (
        expert_down.reshape(hidden_n, hi_count, LO, feat)
        .transpose(2, 0, 1, 3)
        .reshape(LO, hidden_n, wide)
    )
    part = jnp.stack([jnp.dot(hidden, w_down[i], preferred_element_type=F32).astype(BF) for i in range(LO)])
    back = lax.all_to_all(
        part.reshape(LO * ep_count, rows, wide), ("lo", "ep"), 0, 0, tiled=True
    ).reshape(LO * slots, wide)
    mixed = pl.pallas_call(
        functools.partial(combine_kernel, ep_count, rows),
        out_shape=pltpu.VMEM((hi_count, tok_count, feat), BF),
        in_specs=[in_vmem, in_vmem, in_vmem],
        out_specs=in_vmem,
        name="combine",
    )(routing.T, route_gates.T, held_close(back))
    shares = lax.all_to_all(mixed, "hi", 0, 0, tiled=True)
    return jnp.sum(shares.astype(F32), axis=0).astype(BF)


def solution(mesh):
    finer = Mesh(
        mesh.devices.reshape(
            mesh.shape["rep"], mesh.shape["tp"] // LO, LO, mesh.shape["ep"]
        ),
        ("rep", "hi", "lo", "ep"),
    )
    placed = (
        P(REP_EP, TP),
        P(REP_EP, None),
        P(REP_EP, None),
        P("ep", None, TP),
        P("ep", None, TP),
        P("ep", TP, None),
    )
    return jax.shard_map(
        body, mesh=finer, in_specs=placed, out_specs=P(REP_EP, TP), check_vma=False
    )
```

time: 196 us -> 193 us (0.985)
  local copies, waits for them, and re-layouts: 12.8 us -> 9.06 us
  Pallas kernels: 0 us -> 3.72 us
    pallas_call x0 -> x2, Pallas kernels: none -> 3.72 us  [the longest x1 2.36 us: body(): pl.pallas_call(functools.partial(pack_kernel, ep_count, rows), out_shape=...]
    unnamed x17 -> x15, local copies, waits for them, and re-layouts: 5.24 us -> 3.64 us
where the time goes in v3:
time: 193 us; the launch traced here: 192 us
  blocking collectives  155 us (80%)
  waiting for transfers between devices  14.4 us (7%)
  local copies, waits for them, and re-layouts  9.06 us (5%)
  starting transfers between devices  5.88 us (3%)
  Pallas kernels  3.72 us (2%)
  matrix products  2.28 us (1%)
    all_gather x1, blocking collectives, body(): gathered = lax.all_gather(tokens, 'hi', axis=0)  75.1 us
    all_to_all x1, blocking collectives, body(): shares = lax.all_to_all(mixed, 'hi', 0, 0, tiled=True)  55.8 us
    all_to_all x1, blocking collectives, body(): lax.all_to_all(part.reshape(LO * ep_count, rows, wide), ('lo', 'ep'), 0,...  24.2 us
    all_to_all x1, waiting for transfers between devices, body(): lax.all_to_all(sent.reshape(LO * ep_count, rows, wide), ('lo', 'ep'), 0,...  14.4 us
    all_to_all x1, starting transfers between devices, body(): lax.all_to_all(sent.reshape(LO * ep_count, rows, wide), ('lo', 'ep'), 0,...  5.88 us
  transfers between devices with their start and end apart: 1, of which 1 were waited for; matrix products, arithmetic and copies ran while one was open for 4% of the time, Pallas kernels for 0%

profile of v3, /device:TPU:38, one launch (start us, length us, event | category | flops | bytes accessed | tf_op | source)
XLA Modules:
  0.0 191.5 jit_solution(16932640821162990920)
XLA Ops:
  0.0 75.1 %all-gather = bf16[1536,96]{1,0:T(8,128)(2,1)S(1)} all-gather(bf16[96,96]{1,0:T(8,128)(2,1)} %param.6), channel_id=2, replica_groups=mesh['rep'=2,'hi'=16,'lo'=2,'ep'=8] {'hi'}, dimensions={0}, use_global_device_ids=true | all-gather | bytes 313344 | tf_op jit(solution)/shard_map/all_gather | solution.py:71
  75.1 2.4 %pack.1 = bf16[2,256,1536]{2,1,0:T(8,128)(2,1)} custom-call(s32[2,96]{1,0:T(2,128)} %bitcast.55, bf16[16,96,96]{2,1,0:T(8,128)(2,1)S(1)} %bitcast.40), custom_call_target="tpu_custom_call" | custom-call | tf_op jit(solution)/shard_map/pack/pallas_call | solution.py:72
  77.5 5.9 %all-to-all-start = ((bf16[16,32,1536]{2,1,0:T(8,128)(2,1)}), bf16[16,32,1536]{2,1,0:T(8,128)(2,1)S(1)}, u32[]{:S(2)}, u32[]{:S(2)}) async-start(bf16[16,32,1536]{2,1,0:T(8,128)(2,1)} %bitcast.3), calls=%async_computation | async-start | bytes 3145728 | tf_op jit(solution)/shard_map/all_to_all | solution.py:80
  83.4 1.7 copy.7
  85.1 0.0 copy-start.5
  85.1 2.7 %fusion.5 = (bf16[1,16,96,256]{3,2,0,1:T(8,128)(2,1)}, bf16[1,16,96,256]{3,2,0,1:T(8,128)(2,1)}) fusion(bf16[2,16,96,256]{3,2,0,1:T(8,128)(2,1)} %bitcast.52), kind=kLoop, calls=%fused_computation.10 | loop fusion | bytes 3145728 | tf_op jit(solution)/shard_map/slice | solution.py:88
  87.8 0.0 copy-done.5
  87.8 1.3 fusion.6
  89.1 1.3 fusion.4
  90.4 0.0 copy-start
  90.4 14.4 %all-to-all-done = bf16[16,32,1536]{2,1,0:T(8,128)(2,1)S(1)} async-done(((bf16[16,32,1536]{2,1,0:T(8,128)(2,1)}), bf16[16,32,1536]{2,1,0:T(8,128)(2,1)S(1)}, u32[]{:S(2)}, u32[]{:S(2)}) %all-to-all-start) | async-done | bytes 1572896 | tf_op jit(solution)/shard_map/all_to_all | solution.py:80
  104.8 0.1 fusion.7
  104.9 0.0 copy-start.1
  104.9 0.0 copy-done
  104.9 0.0 copy-start.4
  105.0 0.4 fusion.8
  105.3 0.7 copy-done.1
  106.1 0.0 copy-start.6
  106.1 0.4 fusion.9
  106.4 0.0 copy-done.4
  106.4 0.4 convolution_add_fusion.1
  106.8 0.0 copy-start.3
  106.8 0.4 copy-done.6
  107.2 0.4 fusion.3
  107.6 0.0 copy-start.2
  107.6 0.4 copy-done.3
  108.0 0.4 fusion
  108.4 0.4 copy-done.2
  108.8 0.4 fusion.1
  109.2 0.1 pad_maximum_fusion
  109.4 24.2 %all_to_all.15 = bf16[16,32,1536]{2,1,0:T(8,128)(2,1)S(1)} all-to-all(bf16[16,32,1536]{2,1,0:T(8,128)(2,1)S(1)} %bitcast.44), channel_id=1, replica_groups=mesh['rep'=2,'hi'=16,'lo'=2,'ep'=8] {'lo','ep'}, dimensions={0} | all-to-all | bytes 3145728 | tf_op jit(solution)/shard_map/all_to_all | solution.py:98
  133.6 1.4 combine.1
  135.0 55.8 %all_to_all.16 = bf16[16,96,96]{2,1,0:T(8,128)(2,1)S(1)} all-to-all(bf16[16,96,96]{2,1,0:T(8,128)(2,1)S(1)} %combine.1), channel_id=1, replica_groups=mesh['rep'=2,'hi'=16,'lo'=2,'ep'=8] {'hi'}, dimensions={0} | all-to-all | bytes 589824 | tf_op jit(solution)/shard_map/all_to_all | solution.py:108
  190.8 0.7 reduce_sum.12
Async XLA Ops:
  77.5 27.3 %all-to-all-start = ((bf16[16,32,1536]{2,1,0:T(8,128)(2,1)}), bf16[16,32,1536]{2,1,0:T(8,128)(2,1)S(1)}, u32[]{:S(2)}, u32[]{:S(2)}) async-start(bf16[16,32,1536]{2,1,0:T(8,128)(2,1)} %bitcast.3), calls=%async_computation | async-start | bytes 3145728 | tf_op jit(solution)/shard_map/all_to_all | solution.py:80
  85.1 2.8 %copy-start.5 = (bf16[1,3072,256]{2,1,0:T(8,128)(2,1)S(1)}, bf16[1,3072,256]{2,1,0:T(8,128)(2,1)}, u32[]{:S(2)}) copy-start(bf16[1,3072,256]{2,1,0:T(8,128)(2,1)} %param.10) | copy-start | bytes 4718596
  90.4 14.5 %copy-start = (bf16[1,16,96,256]{3,2,0,1:T(8,128)(2,1)S(1)}, bf16[1,16,96,256]{3,2,0,1:T(8,128)(2,1)}, u32[]{:S(2)}) copy-start(bf16[1,16,96,256]{3,2,0,1:T(8,128)(2,1)} %get-tuple-element.8) | copy-start | bytes 2359300
  104.9 1.1 copy-start.1
  104.9 1.5 copy-start.4
  106.1 1.2 copy-start.6
  106.8 1.2 copy-start.3
  107.6 1.2 copy-start.2

commit v4 on v3

--- a/solution.py
+++ b/solution.py
@@ -44,17 +44,23 @@
         out_ref[i] = packed
 
 
-def combine_kernel(experts, rows, routing_ref, gates_ref, back_ref, out_ref):
-    hi_count, _, feat = out_ref.shape
+def combine_kernel(experts, rows, feat, routing_ref, gates_ref, back_ref, out_ref):
+    tok_count = routing_ref.shape[1]
+    hi_count = back_ref.shape[1] // feat
     expert, held = slot_match(routing_ref, experts, rows)
     weight = jnp.where(routing_ref[0:1, :] == expert, gates_ref[0:1, :], gates_ref[1:2, :])
     weight = jnp.where(held, weight, 0.0).astype(BF)
     weight = jnp.concatenate([weight] * LO, axis=0)
     mixed = lax.dot_general(
         weight, back_ref[...], (((0,), (0,)), ((), ())), preferred_element_type=F32
-    ).astype(BF)
+    )
+    full = tok_count * 3 // 4
     for i in range(hi_count):
-        out_ref[i] = mixed[:, i * feat : (i + 1) * feat]
+        at = (i,)
+        block = mixed[:, i * feat : (i + 1) * feat]
+        out_ref[*at, :, :feat] = block[:full].astype(BF)
+        tail = [block[full:, j * (feat // 3) : (j + 1) * (feat // 3)] for j in range(3)]
+        out_ref[*at, :, feat:] = jnp.concatenate(tail, axis=0).astype(BF)
 
 
 def body(tokens, routing, route_gates, expert_gate, expert_up, expert_down):
@@ -99,14 +105,30 @@
         part.reshape(LO * ep_count, rows, wide), ("lo", "ep"), 0, 0, tiled=True
     ).reshape(LO * slots, wide)
     mixed = pl.pallas_call(
-        functools.partial(combine_kernel, ep_count, rows),
-        out_shape=pltpu.VMEM((hi_count, tok_count, feat), BF),
+        functools.partial(combine_kernel, ep_count, rows, feat),
+        out_shape=pltpu.VMEM((*(hi_count,), tok_count * 3 // 4, feat * 4 // 3), BF),
         in_specs=[in_vmem, in_vmem, in_vmem],
         out_specs=in_vmem,
         name="combine",
     )(routing.T, route_gates.T, held_close(back))
     shares = lax.all_to_all(mixed, "hi", 0, 0, tiled=True)
-    return jnp.sum(shares.astype(F32), axis=0).astype(BF)
+    return pl.pallas_call(
+        finish_kernel,
+        out_shape=jax.ShapeDtypeStruct((tok_count, feat), BF),
+        in_specs=[in_vmem],
+        out_specs=in_vmem,
+        name="finish",
+    )(held_close(shares))
+
+
+def finish_kernel(shares_ref, out_ref):
+    tok_count, feat = out_ref.shape
+    full, cut = tok_count * 3 // 4, feat // 3
+    total = jnp.sum(shares_ref[...].astype(F32), axis=0)
+    out_ref[:full] = total[:, :feat].astype(BF)
+    step = full // 3
+    tail = [total[j * step : (j + 1) * step, feat:] for j in range(3)]
+    out_ref[full:] = jnp.concatenate(tail, axis=1).astype(BF)
 
 
 def solution(mesh):

time: 193 us -> 186 us (0.964)
  blocking collectives: 155 us -> 147 us
    all_to_all x1, blocking collectives: 55.8 us -> 47.6 us  [body(): shares = lax.all_to_all(mixed, 'hi', 0, 0, tiled=True)]
where the time goes in v4:
time: 186 us; the launch traced here: 183 us
  blocking collectives  147 us (79%)
  waiting for transfers between devices  14.4 us (8%)
  local copies, waits for them, and re-layouts  9.08 us (5%)
  starting transfers between devices  5.88 us (3%)
  Pallas kernels  4.58 us (2%)
  matrix products  2.28 us (1%)
    all_gather x1, blocking collectives, body(): gathered = lax.all_gather(tokens, 'hi', axis=0)  75.1 us
    all_to_all x1, blocking collectives, body(): shares = lax.all_to_all(mixed, 'hi', 0, 0, tiled=True)  47.6 us
    all_to_all x1, blocking collectives, body(): lax.all_to_all(part.reshape(LO * ep_count, rows, wide), ('lo', 'ep'), 0,...  24.2 us
    all_to_all x1, waiting for transfers between devices, body(): lax.all_to_all(sent.reshape(LO * ep_count, rows, wide), ('lo', 'ep'), 0,...  14.4 us
    all_to_all x1, starting transfers between devices, body(): lax.all_to_all(sent.reshape(LO * ep_count, rows, wide), ('lo', 'ep'), 0,...  5.88 us
  transfers between devices with their start and end apart: 1, of which 1 were waited for; matrix products, arithmetic and copies ran while one was open for 4% of the time, Pallas kernels for 0%

profile of v4, /device:TPU:38, one launch (start us, length us, event | category | flops | bytes accessed | tf_op | source)
XLA Modules:
  0.0 183.5 jit_solution(13250033212636586431)
XLA Ops:
  0.0 75.1 %all-gather = bf16[1536,96]{1,0:T(8,128)(2,1)S(1)} all-gather(bf16[96,96]{1,0:T(8,128)(2,1)} %param.6), channel_id=2, replica_groups=mesh['rep'=2,'hi'=16,'lo'=2,'ep'=8] {'hi'}, dimensions={0}, use_global_device_ids=true | all-gather | bytes 313344 | tf_op jit(solution)/shard_map/all_gather | solution.py:77
  75.1 2.4 %pack.1 = bf16[2,256,1536]{2,1,0:T(8,128)(2,1)} custom-call(s32[2,96]{1,0:T(2,128)} %bitcast.55, bf16[16,96,96]{2,1,0:T(8,128)(2,1)S(1)} %bitcast.40), custom_call_target="tpu_custom_call" | custom-call | tf_op jit(solution)/shard_map/pack/pallas_call | solution.py:78
  77.5 5.9 %all-to-all-start = ((bf16[16,32,1536]{2,1,0:T(8,128)(2,1)}), bf16[16,32,1536]{2,1,0:T(8,128)(2,1)S(1)}, u32[]{:S(2)}, u32[]{:S(2)}) async-start(bf16[16,32,1536]{2,1,0:T(8,128)(2,1)} %bitcast.3), calls=%async_computation | async-start | bytes 3145728 | tf_op jit(solution)/shard_map/all_to_all | solution.py:86
  83.4 1.7 copy.7
  85.1 0.0 copy-start.5
  85.1 2.8 %fusion.5 = (bf16[1,16,96,256]{3,2,0,1:T(8,128)(2,1)}, bf16[1,16,96,256]{3,2,0,1:T(8,128)(2,1)}) fusion(bf16[2,16,96,256]{3,2,0,1:T(8,128)(2,1)} %bitcast.52), kind=kLoop, calls=%fused_computation.10 | loop fusion | bytes 3145728 | tf_op jit(solution)/shard_map/slice | solution.py:94
  87.9 0.0 copy-done.5
  87.9 1.3 fusion.6
  89.2 1.3 fusion.4
  90.5 0.0 copy-start
  90.5 14.4 %all-to-all-done = bf16[16,32,1536]{2,1,0:T(8,128)(2,1)S(1)} async-done(((bf16[16,32,1536]{2,1,0:T(8,128)(2,1)}), bf16[16,32,1536]{2,1,0:T(8,128)(2,1)S(1)}, u32[]{:S(2)}, u32[]{:S(2)}) %all-to-all-start) | async-done | bytes 1572896 | tf_op jit(solution)/shard_map/all_to_all | solution.py:86
  104.8 0.1 fusion.7
  104.9 0.0 copy-start.1
  104.9 0.0 copy-done
  105.0 0.0 copy-start.4
  105.0 0.4 fusion.8
  105.3 0.7 copy-done.1
  106.1 0.0 copy-start.6
  106.1 0.4 fusion.9
  106.5 0.0 copy-done.4
  106.5 0.4 convolution_add_fusion.1
  106.8 0.0 copy-start.3
  106.8 0.4 copy-done.6
  107.3 0.4 fusion.3
  107.6 0.0 copy-start.2
  107.7 0.4 copy-done.3
  108.0 0.4 fusion
  108.4 0.4 copy-done.2
  108.8 0.4 fusion.1
  109.2 0.1 pad_maximum_fusion
  109.4 24.2 %all_to_all.15 = bf16[16,32,1536]{2,1,0:T(8,128)(2,1)S(1)} all-to-all(bf16[16,32,1536]{2,1,0:T(8,128)(2,1)S(1)} %bitcast.44), channel_id=1, replica_groups=mesh['rep'=2,'hi'=16,'lo'=2,'ep'=8] {'lo','ep'}, dimensions={0} | all-to-all | bytes 3145728 | tf_op jit(solution)/shard_map/all_to_all | solution.py:104
  133.7 1.5 combine.1
  135.1 47.6 %all_to_all.16.shares_ref = bf16[16,72,128]{2,1,0:T(8,128)(2,1)S(1)} all-to-all(bf16[16,72,128]{2,1,0:T(8,128)(2,1)S(1)} %combine.1), channel_id=1, replica_groups=mesh['rep'=2,'hi'=16,'lo'=2,'ep'=8] {'hi'}, dimensions={0} | all-to-all | bytes 589824 | tf_op jit(solution)/shard_map/all_to_all | solution.py:114
  182.7 0.7 finish.1
Async XLA Ops:
  77.5 27.3 %all-to-all-start = ((bf16[16,32,1536]{2,1,0:T(8,128)(2,1)}), bf16[16,32,1536]{2,1,0:T(8,128)(2,1)S(1)}, u32[]{:S(2)}, u32[]{:S(2)}) async-start(bf16[16,32,1536]{2,1,0:T(8,128)(2,1)} %bitcast.3), calls=%async_computation | async-start | bytes 3145728 | tf_op jit(solution)/shard_map/all_to_all | solution.py:86
  85.1 2.8 %copy-start.5 = (bf16[1,3072,256]{2,1,0:T(8,128)(2,1)S(1)}, bf16[1,3072,256]{2,1,0:T(8,128)(2,1)}, u32[]{:S(2)}) copy-start(bf16[1,3072,256]{2,1,0:T(8,128)(2,1)} %param.10) | copy-start | bytes 4718596
  90.5 14.5 %copy-start = (bf16[1,16,96,256]{3,2,0,1:T(8,128)(2,1)S(1)}, bf16[1,16,96,256]{3,2,0,1:T(8,128)(2,1)}, u32[]{:S(2)}) copy-start(bf16[1,16,96,256]{3,2,0,1:T(8,128)(2,1)} %get-tuple-element.8) | copy-start | bytes 2359300
  104.9 1.1 copy-start.1
  105.0 1.5 copy-start.4
  106.1 1.2 copy-start.6
  106.8 1.2 copy-start.3
  107.6 1.2 copy-start.2

commit v5 on v4

--- a/solution.py
+++ b/solution.py
@@ -44,6 +44,27 @@
         out_ref[i] = packed
 
 
+def ffn_kernel(got_ref, gate_ref, up_ref, down_ref, out_ref):
+    lo_count = got_ref.shape[0]
+    hi_count, _, feat, hidden_n = gate_ref.shape
+    wide = hi_count * feat
+    gate = up = 0.0
+    for i in range(lo_count):
+        gate += jnp.dot(
+            got_ref[i], gate_ref[:, i].reshape(wide, hidden_n), preferred_element_type=F32
+        )
+        up += jnp.dot(got_ref[i], up_ref[:, i].reshape(wide, hidden_n), preferred_element_type=F32)
+    hidden = (gate / (1.0 + jnp.exp(-gate)) * up).astype(BF)
+    step = 4 * lo_count
+    for k in range(hi_count * lo_count // step):
+        block = jnp.dot(
+            hidden, down_ref[:, k * step * feat : (k + 1) * step * feat], preferred_element_type=F32
+        ).astype(BF)
+        for j in range(step):
+            place = (k * step + j) // lo_count * feat
+            out_ref[j % lo_count, :, place : place + feat] = block[:, j * feat : (j + 1) * feat]
+
+
 def combine_kernel(experts, rows, feat, routing_ref, gates_ref, back_ref, out_ref):
     tok_count = routing_ref.shape[1]
     hi_count = back_ref.shape[1] // feat
@@ -81,26 +102,26 @@
         in_specs=[in_vmem, in_vmem],
         out_specs=in_vmem,
         scratch_shapes=[pltpu.VMEM((tok_count, wide), BF)],
+        compiler_params=pltpu.CompilerParams(vmem_limit_bytes=16 << 20),
         name="pack",
     )(routing.T, held_close(gathered))
     got = lax.all_to_all(
         sent.reshape(LO * ep_count, rows, wide), ("lo", "ep"), 0, 0, tiled=True
     ).reshape(LO, slots, wide)
 
-    def by_lo(w):
-        return w.reshape(hi_count, LO, feat, hidden_n).transpose(1, 0, 2, 3).reshape(LO, wide, hidden_n)
-
-    w_gate, w_up = by_lo(expert_gate), by_lo(expert_up)
-    gate = sum(jnp.dot(got[i], w_gate[i], preferred_element_type=F32) for i in range(LO))
-    up = sum(jnp.dot(got[i], w_up[i], preferred_element_type=F32) for i in range(LO))
-    hidden = (jax.nn.silu(gate) * up).astype(BF)
-
-    w_down = (
-        expert_down.reshape(hidden_n, hi_count, LO, feat)
-        .transpose(2, 0, 1, 3)
-        .reshape(LO, hidden_n, wide)
+    part = pl.pallas_call(
+        ffn_kernel,
+        out_shape=pltpu.VMEM((LO, slots, wide), BF),
+        in_specs=[in_vmem] * 4,
+        out_specs=in_vmem,
+        compiler_params=pltpu.CompilerParams(vmem_limit_bytes=16 << 20),
+        name="ffn",
+    )(
+        held_close(got),
+        held_close(expert_gate.reshape(hi_count, LO, feat, hidden_n)),
+        held_close(expert_up.reshape(hi_count, LO, feat, hidden_n)),
+        held_close(expert_down.reshape(hidden_n, LO * wide)),
     )
-    part = jnp.stack([jnp.dot(hidden, w_down[i], preferred_element_type=F32).astype(BF) for i in range(LO)])
     back = lax.all_to_all(
         part.reshape(LO * ep_count, rows, wide), ("lo", "ep"), 0, 0, tiled=True
     ).reshape(LO * slots, wide)
@@ -109,6 +130,7 @@
         out_shape=pltpu.VMEM((*(hi_count,), tok_count * 3 // 4, feat * 4 // 3), BF),
         in_specs=[in_vmem, in_vmem, in_vmem],
         out_specs=in_vmem,
+        compiler_params=pltpu.CompilerParams(vmem_limit_bytes=16 << 20),
         name="combine",
     )(routing.T, route_gates.T, held_close(back))
     shares = lax.all_to_all(mixed, "hi", 0, 0, tiled=True)
@@ -117,6 +139,7 @@
         out_shape=jax.ShapeDtypeStruct((tok_count, feat), BF),
         in_specs=[in_vmem],
         out_specs=in_vmem,
+        compiler_params=pltpu.CompilerParams(vmem_limit_bytes=16 << 20),
         name="finish",
     )(held_close(shares))
 

time: 186 us -> 182 us (0.978); the launches traced: 183 us -> 182 us
  blocking collectives: 147 us -> 177 us
  waiting for transfers between devices: 14.4 us -> 0 us
  local copies, waits for them, and re-layouts: 9.08 us -> 0.7 us
  starting transfers between devices: 5.88 us -> 0 us
  matrix products: 2.28 us -> 0 us
    all_to_all x0 -> x1, blocking collectives: none -> 25.8 us  [body(): lax.all_to_all(sent.reshape(LO * ep_count, rows, wide), ('lo', 'ep'), 0,...]
    all_to_all x1 -> x0, waiting for transfers between devices: 14.4 us -> none  [body(): lax.all_to_all(sent.reshape(LO * ep_count, rows, wide), ('lo', 'ep'), 0,...]
    all_to_all x1 -> x0, starting transfers between devices: 5.88 us -> none  [body(): lax.all_to_all(sent.reshape(LO * ep_count, rows, wide), ('lo', 'ep'), 0,...]
    slice x4 -> x0, local copies, waits for them, and re-layouts: 5.44 us -> none  [the longest x1 2.76 us: body(): w_gate[i]]
    all_to_all x1, blocking collectives: 47.6 us -> 51.2 us  [body(): shares = lax.all_to_all(mixed, 'hi', 0, 0, tiled=True)]
    unnamed x15 -> x10, local copies, waits for them, and re-layouts: 3.64 us -> 0.7 us
    dot_general x6 -> x0, matrix products: 2.28 us -> none  [the longest x2 0.8 us: body(): jnp.dot(hidden, w_down[i], preferred_element_type=F32).astype(BF)]
    pallas_call x0 -> x1, Pallas kernels: none -> 2 us  [body(): pl.pallas_call(ffn_kernel, out_shape=pltpu.VMEM((LO, slots, wide), BF), i...]
  transfers between devices with their start and end apart: 1 -> 0, of which waited for: 1 -> 0; matrix products, arithmetic and copies ran while one was open for 4% -> 0% of each run, Pallas kernels for 0% -> 0%
where the time goes in v5:
time: 182 us
  blocking collectives  177 us (97%)
  Pallas kernels  4.05 us (2%)
    all_gather x1, blocking collectives, body(): gathered = lax.all_gather(tokens, 'hi', axis=0)  75.1 us
    all_to_all x1, blocking collectives, body(): shares = lax.all_to_all(mixed, 'hi', 0, 0, tiled=True)  51.2 us
    all_to_all x1, blocking collectives, body(): lax.all_to_all(sent.reshape(LO * ep_count, rows, wide), ('lo', 'ep'), 0,...  25.8 us
    all_to_all x1, blocking collectives, body(): lax.all_to_all(part.reshape(LO * ep_count, rows, wide), ('lo', 'ep'), 0,...  24.8 us

profile of v5, /device:TPU:38, one launch (start us, length us, event | category | flops | bytes accessed | tf_op | source)
XLA Modules:
  0.0 181.7 jit_solution(1836394608359913816)
XLA Ops:
  0.0 75.1 %all-gather = bf16[1536,96]{1,0:T(8,128)(2,1)S(1)} all-gather(bf16[96,96]{1,0:T(8,128)(2,1)} %param.6), channel_id=2, replica_groups=mesh['rep'=2,'hi'=16,'lo'=2,'ep'=8] {'hi'}, dimensions={0}, use_global_device_ids=true | all-gather | bytes 313344 | tf_op jit(solution)/shard_map/all_gather | solution.py:98
  75.1 0.0 copy-start.3
  75.1 0.7 copy-done.3
  75.8 0.0 copy-start.2
  75.8 0.5 pack.1
  76.4 0.0 copy-start
  76.4 0.0 copy-start.1
  76.4 25.8 %all_to_all.15 = bf16[16,32,1536]{2,1,0:T(8,128)(2,1)S(1)} all-to-all(bf16[16,32,1536]{2,1,0:T(8,128)(2,1)S(1)} %bitcast.10), channel_id=1, replica_groups=mesh['rep'=2,'hi'=16,'lo'=2,'ep'=8] {'lo','ep'}, dimensions={0} | all-to-all | bytes 3145728 | tf_op jit(solution)/shard_map/all_to_all | solution.py:108
  102.1 0.0 copy-done.2
  102.1 0.0 copy-done
  102.2 0.0 copy-done.1
  102.2 2.0 %ffn.1 = bf16[2,256,1536]{2,1,0:T(8,128)(2,1)S(1)} custom-call(bf16[2,256,1536]{2,1,0:T(8,128)(2,1)S(1)} %bitcast.12, bf16[16,2,96,256]{3,2,1,0:T(8,128)(2,1)S(1)} %bitcast.15, bf16[16,2,96,256]{3,2,1,0:T(8,128)(2,1)S(1)} %bitcast.16, bf16[256,3072]{1,0:T(8,128)(2,1)S(1)} %bitcast.17), custom_call_target="tpu_custom_call" | custom-call | tf_op jit(solution)/shard_map/ffn/pallas_call | solution.py:112
  104.2 0.0 copy-start.4
  104.2 24.8 %all_to_all.16 = bf16[16,32,1536]{2,1,0:T(8,128)(2,1)S(1)} all-to-all(bf16[16,32,1536]{2,1,0:T(8,128)(2,1)S(1)} %bitcast.13), channel_id=1, replica_groups=mesh['rep'=2,'hi'=16,'lo'=2,'ep'=8] {'lo','ep'}, dimensions={0} | all-to-all | bytes 3145728 | tf_op jit(solution)/shard_map/all_to_all | solution.py:125
  129.0 0.0 copy-done.4
  129.0 0.8 combine.1
  129.8 51.2 %all_to_all.17.shares_ref = bf16[16,72,128]{2,1,0:T(8,128)(2,1)S(1)} all-to-all(bf16[16,72,128]{2,1,0:T(8,128)(2,1)S(1)} %combine.1), channel_id=1, replica_groups=mesh['rep'=2,'hi'=16,'lo'=2,'ep'=8] {'hi'}, dimensions={0} | all-to-all | bytes 589824 | tf_op jit(solution)/shard_map/all_to_all | solution.py:136
  181.0 0.7 finish.1
Async XLA Ops:
  75.1 0.7 copy-start.3
  75.8 26.3 %copy-start.2 = (bf16[1,256,3072]{2,1,0:T(8,128)(2,1)S(1)}, bf16[1,256,3072]{2,1,0:T(8,128)(2,1)}, u32[]{:S(2)}) copy-start(bf16[1,256,3072]{2,1,0:T(8,128)(2,1)} %param.11) | copy-start | bytes 4718596
  76.4 25.8 %copy-start = (bf16[1,3072,256]{2,1,0:T(8,128)(2,1)S(1)}, bf16[1,3072,256]{2,1,0:T(8,128)(2,1)}, u32[]{:S(2)}) copy-start(bf16[1,3072,256]{2,1,0:T(8,128)(2,1)} %param.9) | copy-start | bytes 4718596
  76.4 25.8 %copy-start.1 = (bf16[1,3072,256]{2,1,0:T(8,128)(2,1)S(1)}, bf16[1,3072,256]{2,1,0:T(8,128)(2,1)}, u32[]{:S(2)}) copy-start(bf16[1,3072,256]{2,1,0:T(8,128)(2,1)} %param.10) | copy-start | bytes 4718596
  104.2 24.8 %copy-start.4 = (f32[96,2]{0,1:T(2,128)S(1)}, f32[96,2]{0,1:T(2,128)}, u32[]{:S(2)}) copy-start(f32[96,2]{0,1:T(2,128)} %param.8) | copy-start | bytes 2308

commit v6 on v5

--- a/solution.py
+++ b/solution.py
@@ -9,7 +9,8 @@
 from jax.sharding import PartitionSpec as P
 
 REP_EP = ("rep", "ep")
-TP = ("hi", "lo")
+HI = ("h3", "h2", "h1", "h0")
+TP = (*HI, "lo")
 BF = jnp.bfloat16
 F32 = jnp.float32
 LO = 2
@@ -17,6 +18,14 @@
 
 def held_close(value):
     return pltpu.with_memory_space_constraint(value, pltpu.VMEM)
+
+
+ORDER = (1, 0, 3, 2)
+
+
+def mirrored(index):
+    bits = f"{index:0{len(HI)}b}"
+    return int("".join(bits[i] for i in ORDER), 2)
 
 
 def slot_match(routing_ref, experts, rows):
@@ -77,16 +86,16 @@
     )
     full = tok_count * 3 // 4
     for i in range(hi_count):
-        at = (i,)
+        at = mirrored(i)
         block = mixed[:, i * feat : (i + 1) * feat]
-        out_ref[*at, :, :feat] = block[:full].astype(BF)
+        out_ref[at, :, :feat] = block[:full].astype(BF)
         tail = [block[full:, j * (feat // 3) : (j + 1) * (feat // 3)] for j in range(3)]
-        out_ref[*at, :, feat:] = jnp.concatenate(tail, axis=0).astype(BF)
+        out_ref[at, :, feat:] = jnp.concatenate(tail, axis=0).astype(BF)
 
 
 def body(tokens, routing, route_gates, expert_gate, expert_up, expert_down):
     ep_count = lax.axis_size("ep")
-    hi_count = lax.axis_size("hi")
+    hi_count = lax.axis_size(HI)
     tok_count, feat = tokens.shape
     capacity = 2 * tok_count // ep_count + tok_count // 16
     rows = -(-capacity // 16) * 16
@@ -95,7 +104,7 @@
     hidden_n = expert_gate.shape[2]
     in_vmem = pl.BlockSpec(memory_space=pltpu.VMEM)
 
-    gathered = lax.all_gather(tokens, "hi", axis=0)
+    gathered = lax.all_gather(tokens, HI, axis=0)
     sent = pl.pallas_call(
         functools.partial(pack_kernel, ep_count, rows),
         out_shape=pltpu.VMEM((LO, slots, wide), BF),
@@ -127,13 +136,13 @@
     ).reshape(LO * slots, wide)
     mixed = pl.pallas_call(
         functools.partial(combine_kernel, ep_count, rows, feat),
-        out_shape=pltpu.VMEM((*(hi_count,), tok_count * 3 // 4, feat * 4 // 3), BF),
+        out_shape=pltpu.VMEM((hi_count, tok_count * 3 // 4, feat * 4 // 3), BF),
         in_specs=[in_vmem, in_vmem, in_vmem],
         out_specs=in_vmem,
         compiler_params=pltpu.CompilerParams(vmem_limit_bytes=16 << 20),
         name="combine",
     )(routing.T, route_gates.T, held_close(back))
-    shares = lax.all_to_all(mixed, "hi", 0, 0, tiled=True)
+    shares = lax.all_to_all(mixed, tuple(HI[i] for i in ORDER), 0, 0, tiled=True)
     return pl.pallas_call(
         finish_kernel,
         out_shape=jax.ShapeDtypeStruct((tok_count, feat), BF),
@@ -157,9 +166,9 @@
 def solution(mesh):
     finer = Mesh(
         mesh.devices.reshape(
-            mesh.shape["rep"], mesh.shape["tp"] // LO, LO, mesh.shape["ep"]
+            mesh.shape["rep"], *[2] * len(HI), LO, mesh.shape["ep"]
         ),
-        ("rep", "hi", "lo", "ep"),
+        ("rep", *TP, "ep"),
     )
     placed = (
         P(REP_EP, TP),

time: 182 us -> 178 us (0.978); the launches traced: 182 us -> 175 us
  blocking collectives: 177 us -> 170 us
    all_to_all x1, blocking collectives: 51.2 us -> 44.6 us  [body(): lax.all_to_all(mixed, tuple((HI[i] for i in ORDER)), 0, 0, tiled=True)]
where the time goes in v6:
time: 178 us; the launch traced here: 175 us
  blocking collectives  170 us (96%)
  Pallas kernels  4.05 us (2%)
    all_gather x1, blocking collectives, body(): gathered = lax.all_gather(tokens, HI, axis=0)  75.1 us
    all_to_all x1, blocking collectives, body(): lax.all_to_all(mixed, tuple((HI[i] for i in ORDER)), 0, 0, tiled=True)  44.6 us
    all_to_all x1, blocking collectives, body(): lax.all_to_all(sent.reshape(LO * ep_count, rows, wide), ('lo', 'ep'), 0,...  25.8 us
    all_to_all x1, blocking collectives, body(): lax.all_to_all(part.reshape(LO * ep_count, rows, wide), ('lo', 'ep'), 0,...  24.8 us

profile of v6, /device:TPU:38, one launch (start us, length us, event | category | flops | bytes accessed | tf_op | source)
XLA Modules:
  0.0 175.1 jit_solution(15407718065286826755)
XLA Ops:
  0.0 75.1 %all-gather = bf16[1536,96]{1,0:T(8,128)(2,1)S(1)} all-gather(bf16[96,96]{1,0:T(8,128)(2,1)} %param.6), channel_id=2, replica_groups=mesh['rep'=2,'h3'=2,'h2'=2,'h1'=2,'h0'=2,'lo'=2,'ep'=8] {'h3','h2','h1',..., dimensions={0}, use_global_device_ids=true | all-gather | bytes 313344 | tf_op jit(solution)/shard_map/all_gather | solution.py:107
  75.1 0.0 copy-start.3
  75.1 0.7 copy-done.3
  75.8 0.0 copy-start.2
  75.8 0.5 pack.1
  76.4 0.0 copy-start
  76.4 0.0 copy-start.1
  76.4 25.8 %all_to_all.15 = bf16[16,32,1536]{2,1,0:T(8,128)(2,1)S(1)} all-to-all(bf16[16,32,1536]{2,1,0:T(8,128)(2,1)S(1)} %bitcast.10), channel_id=1, replica_groups=mesh['rep'=2,'h3'=2,'h2'=2,'h1'=2,'h0'=2,'lo'=2,'ep'=8] {'lo','ep'}, dimensions={0} | all-to-all | bytes 3145728 | tf_op jit(solution)/shard_map/all_to_all | solution.py:117
  102.1 0.0 copy-done.2
  102.1 0.0 copy-done
  102.2 0.0 copy-done.1
  102.2 2.0 %ffn.1 = bf16[2,256,1536]{2,1,0:T(8,128)(2,1)S(1)} custom-call(bf16[2,256,1536]{2,1,0:T(8,128)(2,1)S(1)} %bitcast.12, bf16[16,2,96,256]{3,2,1,0:T(8,128)(2,1)S(1)} %bitcast.15, bf16[16,2,96,256]{3,2,1,0:T(8,128)(2,1)S(1)} %bitcast.16, bf16[256,3072]{1,0:T(8,128)(2,1)S(1)} %bitcast.17), custom_call_target="tpu_custom_call" | custom-call | tf_op jit(solution)/shard_map/ffn/pallas_call | solution.py:121
  104.2 0.0 copy-start.4
  104.2 24.8 %all_to_all.16 = bf16[16,32,1536]{2,1,0:T(8,128)(2,1)S(1)} all-to-all(bf16[16,32,1536]{2,1,0:T(8,128)(2,1)S(1)} %bitcast.13), channel_id=1, replica_groups=mesh['rep'=2,'h3'=2,'h2'=2,'h1'=2,'h0'=2,'lo'=2,'ep'=8] {'lo','ep'}, dimensions={0} | all-to-all | bytes 3145728 | tf_op jit(solution)/shard_map/all_to_all | solution.py:134
  129.0 0.0 copy-done.4
  129.0 0.8 combine.1
  129.8 44.6 %all_to_all.17.shares_ref = bf16[16,72,128]{2,1,0:T(8,128)(2,1)S(1)} all-to-all(bf16[16,72,128]{2,1,0:T(8,128)(2,1)S(1)} %combine.1), channel_id=1, replica_groups=mesh['rep'=2,'h3'=2,'h2'=2,'h1'=2,'h0'=2,'lo'=2,'ep'=8] {'h2','h3','h0',..., dimensions={0} | all-to-all | bytes 589824 | tf_op jit(solution)/shard_map/all_to_all | solution.py:145
  174.4 0.7 finish.1
Async XLA Ops:
  75.1 0.7 copy-start.3
  75.8 26.3 %copy-start.2 = (bf16[1,256,3072]{2,1,0:T(8,128)(2,1)S(1)}, bf16[1,256,3072]{2,1,0:T(8,128)(2,1)}, u32[]{:S(2)}) copy-start(bf16[1,256,3072]{2,1,0:T(8,128)(2,1)} %param.11) | copy-start | bytes 4718596
  76.4 25.8 %copy-start = (bf16[1,3072,256]{2,1,0:T(8,128)(2,1)S(1)}, bf16[1,3072,256]{2,1,0:T(8,128)(2,1)}, u32[]{:S(2)}) copy-start(bf16[1,3072,256]{2,1,0:T(8,128)(2,1)} %param.9) | copy-start | bytes 4718596
  76.4 25.8 %copy-start.1 = (bf16[1,3072,256]{2,1,0:T(8,128)(2,1)S(1)}, bf16[1,3072,256]{2,1,0:T(8,128)(2,1)}, u32[]{:S(2)}) copy-start(bf16[1,3072,256]{2,1,0:T(8,128)(2,1)} %param.10) | copy-start | bytes 4718596
  104.2 24.8 %copy-start.4 = (f32[96,2]{0,1:T(2,128)S(1)}, f32[96,2]{0,1:T(2,128)}, u32[]{:S(2)}) copy-start(f32[96,2]{0,1:T(2,128)} %param.8) | copy-start | bytes 2308

commit v7 on v6

--- a/solution.py
+++ b/solution.py
@@ -42,47 +42,74 @@
     return expert, named & (before == place.astype(F32))
 
 
+def folded(value, full):
+    part, step = value.shape[1] // 4, full // 4
+    tail = [value[full : full + step, i * part : (i + 1) * part] for i in range(4)]
+    return jnp.concatenate([value[:full], jnp.concatenate(tail, axis=0)], axis=1).astype(BF)
+
+
+def unfolded(value, rows):
+    full, part = value.shape[0], value.shape[1] // 5
+    step = full // 4
+    value = value.astype(F32)
+    tail = [value[i * step : (i + 1) * step, 4 * part :] for i in range(4)]
+    spare = jnp.zeros((rows - full - step, 4 * part), F32)
+    return jnp.concatenate(
+        [value[:, : 4 * part], jnp.concatenate([jnp.concatenate(tail, axis=1), spare], axis=0)], axis=0
+    ).astype(BF)
+
+
 def pack_kernel(experts, rows, routing_ref, tokens_ref, out_ref, whole_ref):
     hi_count, _, feat = tokens_ref.shape
     _, held = slot_match(routing_ref, experts, rows)
     dispatch = held.astype(F32).astype(BF)
     for i in range(hi_count):
         whole_ref[:, i * feat : (i + 1) * feat] = tokens_ref[i]
-    packed = jnp.dot(dispatch, whole_ref[...], preferred_element_type=F32).astype(BF)
-    for i in range(out_ref.shape[0]):
-        out_ref[i] = packed
-
-
-def ffn_kernel(got_ref, gate_ref, up_ref, down_ref, out_ref):
-    lo_count = got_ref.shape[0]
+    packed = jnp.dot(dispatch, whole_ref[...], preferred_element_type=F32)
+    for e in range(experts):
+        piece = folded(packed[e * rows : (e + 1) * rows], out_ref.shape[2])
+        for i in range(out_ref.shape[0]):
+            out_ref[i, e] = piece
+
+
+def ffn_kernel(rows, got_ref, gate_ref, up_ref, down_ref, out_ref, got_rows, part_rows):
+    lo_count, experts, full, _ = got_ref.shape
+    for i in range(lo_count):
+        for e in range(experts):
+            got_rows[i, e * rows : (e + 1) * rows] = unfolded(got_ref[i, e], rows)
     hi_count, _, feat, hidden_n = gate_ref.shape
     wide = hi_count * feat
     gate = up = 0.0
     for i in range(lo_count):
         gate += jnp.dot(
-            got_ref[i], gate_ref[:, i].reshape(wide, hidden_n), preferred_element_type=F32
+            got_rows[i], gate_ref[:, i].reshape(wide, hidden_n), preferred_element_type=F32
         )
-        up += jnp.dot(got_ref[i], up_ref[:, i].reshape(wide, hidden_n), preferred_element_type=F32)
+        up += jnp.dot(got_rows[i], up_ref[:, i].reshape(wide, hidden_n), preferred_element_type=F32)
     hidden = (gate / (1.0 + jnp.exp(-gate)) * up).astype(BF)
     step = 4 * lo_count
     for k in range(hi_count * lo_count // step):
         block = jnp.dot(
             hidden, down_ref[:, k * step * feat : (k + 1) * step * feat], preferred_element_type=F32
-        ).astype(BF)
+        )
         for j in range(step):
             place = (k * step + j) // lo_count * feat
-            out_ref[j % lo_count, :, place : place + feat] = block[:, j * feat : (j + 1) * feat]
-
-
-def combine_kernel(experts, rows, feat, routing_ref, gates_ref, back_ref, out_ref):
+            part_rows[j % lo_count, :, place : place + feat] = block[:, j * feat : (j + 1) * feat]
+    for i in range(lo_count):
+        for e in range(experts):
+            out_ref[i, e] = folded(part_rows[i, e * rows : (e + 1) * rows], full)
+
+
+def combine_kernel(experts, rows, feat, routing_ref, gates_ref, back_ref, out_ref, back_rows):
     tok_count = routing_ref.shape[1]
-    hi_count = back_ref.shape[1] // feat
+    hi_count = back_rows.shape[1] // feat
+    for i in range(LO * experts):
+        back_rows[i * rows : (i + 1) * rows] = unfolded(back_ref[i], rows)
     expert, held = slot_match(routing_ref, experts, rows)
     weight = jnp.where(routing_ref[0:1, :] == expert, gates_ref[0:1, :], gates_ref[1:2, :])
     weight = jnp.where(held, weight, 0.0).astype(BF)
     weight = jnp.concatenate([weight] * LO, axis=0)
     mixed = lax.dot_general(
-        weight, back_ref[...], (((0,), (0,)), ((), ())), preferred_element_type=F32
+        weight, back_rows[...], (((0,), (0,)), ((), ())), preferred_element_type=F32
     )
     full = tok_count * 3 // 4
     for i in range(hi_count):
@@ -101,13 +128,15 @@
     rows = -(-capacity // 16) * 16
     slots = ep_count * rows
     wide = hi_count * feat
+    full = capacity * 4 // 5
+    piece = (full, wide * 5 // 4)
     hidden_n = expert_gate.shape[2]
     in_vmem = pl.BlockSpec(memory_space=pltpu.VMEM)
 
     gathered = lax.all_gather(tokens, HI, axis=0)
     sent = pl.pallas_call(
         functools.partial(pack_kernel, ep_count, rows),
-        out_shape=pltpu.VMEM((LO, slots, wide), BF),
+        out_shape=pltpu.VMEM((LO, ep_count, *piece), BF),
         in_specs=[in_vmem, in_vmem],
         out_specs=in_vmem,
         scratch_shapes=[pltpu.VMEM((tok_count, wide), BF)],
@@ -115,14 +144,15 @@
         name="pack",
     )(routing.T, held_close(gathered))
     got = lax.all_to_all(
-        sent.reshape(LO * ep_count, rows, wide), ("lo", "ep"), 0, 0, tiled=True
-    ).reshape(LO, slots, wide)
+        sent.reshape(LO * ep_count, *piece), ("lo", "ep"), 0, 0, tiled=True
+    ).reshape(LO, ep_count, *piece)
 
     part = pl.pallas_call(
-        ffn_kernel,
-        out_shape=pltpu.VMEM((LO, slots, wide), BF),
+        functools.partial(ffn_kernel, rows),
+        out_shape=pltpu.VMEM((LO, ep_count, *piece), BF),
         in_specs=[in_vmem] * 4,
         out_specs=in_vmem,
+        scratch_shapes=[pltpu.VMEM((LO, slots, wide), BF), pltpu.VMEM((LO, slots, wide), F32)],
         compiler_params=pltpu.CompilerParams(vmem_limit_bytes=16 << 20),
         name="ffn",
     )(
@@ -132,13 +162,14 @@
         held_close(expert_down.reshape(hidden_n, LO * wide)),
     )
     back = lax.all_to_all(
-        part.reshape(LO * ep_count, rows, wide), ("lo", "ep"), 0, 0, tiled=True
-    ).reshape(LO * slots, wide)
+        part.reshape(LO * ep_count, *piece), ("lo", "ep"), 0, 0, tiled=True
+    )
     mixed = pl.pallas_call(
         functools.partial(combine_kernel, ep_count, rows, feat),
         out_shape=pltpu.VMEM((hi_count, tok_count * 3 // 4, feat * 4 // 3), BF),
         in_specs=[in_vmem, in_vmem, in_vmem],
         out_specs=in_vmem,
+        scratch_shapes=[pltpu.VMEM((LO * slots, wide), BF)],
         compiler_params=pltpu.CompilerParams(vmem_limit_bytes=16 << 20),
         name="combine",
     )(routing.T, route_gates.T, held_close(back))

time: 178 us -> 177 us (level)
  blocking collectives: 170 us -> 168 us
    all_to_all x2, blocking collectives: 50.6 us -> 48.5 us  [the longest x1 24.7 us: body(): lax.all_to_all(sent.reshape(LO * ep_count, *piece), ('lo', 'ep'), 0, 0, t...]
where the time goes in v7:
time: 177 us; the launch traced here: 174 us
  blocking collectives  168 us (95%)
  Pallas kernels  4.66 us (3%)
    all_gather x1, blocking collectives, body(): gathered = lax.all_gather(tokens, HI, axis=0)  75.1 us
    all_to_all x1, blocking collectives, body(): lax.all_to_all(mixed, tuple((HI[i] for i in ORDER)), 0, 0, tiled=True)  44.6 us
    all_to_all x1, blocking collectives, body(): lax.all_to_all(sent.reshape(LO * ep_count, *piece), ('lo', 'ep'), 0, 0, t...  24.7 us
    all_to_all x1, blocking collectives, body(): lax.all_to_all(part.reshape(LO * ep_count, *piece), ('lo', 'ep'), 0, 0, t...  23.8 us

profile of v7, /device:TPU:38, one launch (start us, length us, event | category | flops | bytes accessed | tf_op | source)
XLA Modules:
  0.0 173.6 jit_solution(4366948307806996693)
XLA Ops:
  0.0 75.1 %all-gather = bf16[1536,96]{1,0:T(8,128)(2,1)S(1)} all-gather(bf16[96,96]{1,0:T(8,128)(2,1)} %param.6), channel_id=2, replica_groups=mesh['rep'=2,'h3'=2,'h2'=2,'h1'=2,'h0'=2,'lo'=2,'ep'=8] {'h3','h2','h1',..., dimensions={0}, use_global_device_ids=true | all-gather | bytes 313344 | tf_op jit(solution)/shard_map/all_gather | solution.py:136
  75.1 0.0 copy-start.3
  75.1 0.7 copy-done.3
  75.8 0.0 copy-start.1
  75.8 0.0 copy-start.2
  75.8 0.5 pack.1
  76.4 0.0 copy-start
  76.4 24.7 %all_to_all.15 = bf16[16,24,1920]{2,1,0:T(8,128)(2,1)S(1)} all-to-all(bf16[16,24,1920]{2,1,0:T(8,128)(2,1)S(1)} %bitcast.9), channel_id=1, replica_groups=mesh['rep'=2,'h3'=2,'h2'=2,'h1'=2,'h0'=2,'lo'=2,'ep'=8] {'lo','ep'}, dimensions={0} | all-to-all | bytes 2949120 | tf_op jit(solution)/shard_map/all_to_all | solution.py:146
  101.1 0.0 copy-done.1
  101.1 0.0 copy-done.2
  101.1 0.0 copy-done
  101.1 2.6 %ffn.1 = bf16[2,8,24,1920]{3,2,1,0:T(8,128)(2,1)S(1)} custom-call(bf16[2,8,24,1920]{3,2,1,0:T(8,128)(2,1)S(1)} %bitcast.10, bf16[16,2,96,256]{3,2,1,0:T(8,128)(2,1)S(1)} %bitcast.13, bf16[16,2,96,256]{3,2,1,0:T(8,128)(2,1)S(1)} %bitcast.14, bf16[256,3072]{1,0:T(8,128)(2,1)S(1)} %bitcast.15), custom_call_target="tpu_custom_call" | custom-call | tf_op jit(solution)/shard_map/ffn/pallas_call | solution.py:150
  103.7 0.0 copy-start.4
  103.7 23.8 %all_to_all.16.back_ref = bf16[16,24,1920]{2,1,0:T(8,128)(2,1)S(1)} all-to-all(bf16[16,24,1920]{2,1,0:T(8,128)(2,1)S(1)} %bitcast.11), channel_id=1, replica_groups=mesh['rep'=2,'h3'=2,'h2'=2,'h1'=2,'h0'=2,'lo'=2,'ep'=8] {'lo','ep'}, dimensions={0} | all-to-all | bytes 2949120 | tf_op jit(solution)/shard_map/all_to_all | solution.py:164
  127.5 0.0 copy-done.4
  127.5 0.8 combine.1
  128.3 44.6 %all_to_all.17.shares_ref = bf16[16,72,128]{2,1,0:T(8,128)(2,1)S(1)} all-to-all(bf16[16,72,128]{2,1,0:T(8,128)(2,1)S(1)} %combine.1), channel_id=1, replica_groups=mesh['rep'=2,'h3'=2,'h2'=2,'h1'=2,'h0'=2,'lo'=2,'ep'=8] {'h2','h3','h0',..., dimensions={0} | all-to-all | bytes 589824 | tf_op jit(solution)/shard_map/all_to_all | solution.py:176
  172.9 0.7 finish.1
Async XLA Ops:
  75.1 0.7 copy-start.3
  75.8 25.2 %copy-start.1 = (bf16[1,3072,256]{2,1,0:T(8,128)(2,1)S(1)}, bf16[1,3072,256]{2,1,0:T(8,128)(2,1)}, u32[]{:S(2)}) copy-start(bf16[1,3072,256]{2,1,0:T(8,128)(2,1)} %param.10) | copy-start | bytes 4718596
  75.8 25.2 %copy-start.2 = (bf16[1,256,3072]{2,1,0:T(8,128)(2,1)S(1)}, bf16[1,256,3072]{2,1,0:T(8,128)(2,1)}, u32[]{:S(2)}) copy-start(bf16[1,256,3072]{2,1,0:T(8,128)(2,1)} %param.11) | copy-start | bytes 4718596
  76.4 24.7 %copy-start = (bf16[1,3072,256]{2,1,0:T(8,128)(2,1)S(1)}, bf16[1,3072,256]{2,1,0:T(8,128)(2,1)}, u32[]{:S(2)}) copy-start(bf16[1,3072,256]{2,1,0:T(8,128)(2,1)} %param.9) | copy-start | bytes 4718596
  103.7 23.8 %copy-start.4 = (f32[96,2]{0,1:T(2,128)S(1)}, f32[96,2]{0,1:T(2,128)}, u32[]{:S(2)}) copy-start(f32[96,2]{0,1:T(2,128)} %param.8) | copy-start | bytes 2308

commit v8 on v7

--- a/solution.py
+++ b/solution.py
@@ -20,12 +20,11 @@
     return pltpu.with_memory_space_constraint(value, pltpu.VMEM)
 
 
-ORDER = (1, 0, 3, 2)
+ORDER = [0, 3, 1, 2, 8, 11, 9, 10, 4, 7, 5, 6, 12, 15, 13, 14]
 
 
 def mirrored(index):
-    bits = f"{index:0{len(HI)}b}"
-    return int("".join(bits[i] for i in ORDER), 2)
+    return ORDER.index(index)
 
 
 def slot_match(routing_ref, experts, rows):
@@ -59,13 +58,19 @@
     ).astype(BF)
 
 
-def pack_kernel(experts, rows, routing_ref, tokens_ref, out_ref, whole_ref):
+def stage_kernel(experts, rows, routing_ref, tokens_ref, held_ref, out_ref, sem):
+    copy = pltpu.make_async_copy(tokens_ref, out_ref, sem)
+    copy.start()
+    _, held = slot_match(routing_ref, experts, rows)
+    held_ref[...] = held.astype(F32).astype(BF)
+    copy.wait()
+
+
+def pack_kernel(experts, rows, dispatch_ref, tokens_ref, out_ref, whole_ref):
     hi_count, _, feat = tokens_ref.shape
-    _, held = slot_match(routing_ref, experts, rows)
-    dispatch = held.astype(F32).astype(BF)
     for i in range(hi_count):
         whole_ref[:, i * feat : (i + 1) * feat] = tokens_ref[i]
-    packed = jnp.dot(dispatch, whole_ref[...], preferred_element_type=F32)
+    packed = jnp.dot(dispatch_ref[...], whole_ref[...], preferred_element_type=F32)
     for e in range(experts):
         piece = folded(packed[e * rows : (e + 1) * rows], out_ref.shape[2])
         for i in range(out_ref.shape[0]):
@@ -133,7 +138,16 @@
     hidden_n = expert_gate.shape[2]
     in_vmem = pl.BlockSpec(memory_space=pltpu.VMEM)
 
-    gathered = lax.all_gather(tokens, HI, axis=0)
+    dispatch, staged = pl.pallas_call(
+        functools.partial(stage_kernel, ep_count, rows),
+        out_shape=(pltpu.VMEM((slots, tok_count), BF), pltpu.VMEM((tok_count, feat), BF)),
+        in_specs=[in_vmem, pl.BlockSpec(memory_space=pl.ANY)],
+        out_specs=(in_vmem, in_vmem),
+        scratch_shapes=[pltpu.SemaphoreType.DMA],
+        compiler_params=pltpu.CompilerParams(vmem_limit_bytes=16 << 20),
+        name="stage",
+    )(routing.T, pltpu.with_memory_space_constraint(tokens, pltpu.HBM))
+    gathered = lax.all_gather(staged, HI, axis=0)
     sent = pl.pallas_call(
         functools.partial(pack_kernel, ep_count, rows),
         out_shape=pltpu.VMEM((LO, ep_count, *piece), BF),
@@ -142,7 +156,7 @@
         scratch_shapes=[pltpu.VMEM((tok_count, wide), BF)],
         compiler_params=pltpu.CompilerParams(vmem_limit_bytes=16 << 20),
         name="pack",
-    )(routing.T, held_close(gathered))
+    )(held_close(dispatch), held_close(gathered))
     got = lax.all_to_all(
         sent.reshape(LO * ep_count, *piece), ("lo", "ep"), 0, 0, tiled=True
     ).reshape(LO, ep_count, *piece)
@@ -173,7 +187,7 @@
         compiler_params=pltpu.CompilerParams(vmem_limit_bytes=16 << 20),
         name="combine",
     )(routing.T, route_gates.T, held_close(back))
-    shares = lax.all_to_all(mixed, tuple(HI[i] for i in ORDER), 0, 0, tiled=True)
+    shares = lax.all_to_all(mixed, TP, 0, 0, tiled=True, axis_index_groups=[[LO * i + j for i in ORDER] for j in range(LO)])
     return pl.pallas_call(
         finish_kernel,
         out_shape=jax.ShapeDtypeStruct((tok_count, feat), BF),

time: 177 us -> 177 us (level); the launches traced: 174 us -> 176 us
  blocking collectives: 168 us -> 170 us
where the time goes in v8:
time: 177 us; the launch traced here: 176 us
  blocking collectives  170 us (96%)
  Pallas kernels  5.35 us (3%)
    all_gather x1, blocking collectives, body(): gathered = lax.all_gather(staged, HI, axis=0)  75 us
    all_to_all x1, blocking collectives, body(): lax.all_to_all(mixed, TP, 0, 0, tiled=True, axis_index_groups=[[LO * i +...  46.3 us
    all_to_all x1, blocking collectives, body(): lax.all_to_all(sent.reshape(LO * ep_count, *piece), ('lo', 'ep'), 0, 0, t...  24.6 us
    all_to_all x1, blocking collectives, body(): lax.all_to_all(part.reshape(LO * ep_count, *piece), ('lo', 'ep'), 0, 0, t...  23.8 us

profile of v8, /device:TPU:38, one launch (start us, length us, event | category | flops | bytes accessed | tf_op | source)
XLA Modules:
  0.0 175.7 jit_solution(4508229191968782920)
XLA Ops:
  0.0 0.0 copy-start.3
  0.0 0.7 copy-done.3
  0.7 0.7 stage.1
  1.4 75.0 %all-gather = bf16[1536,96]{1,0:T(8,128)(2,1)S(1)} all-gather(bf16[96,96]{1,0:T(8,128)(2,1)S(1)} %get-tuple-element.8), channel_id=2, replica_groups=mesh['rep'=2,'h3'=2,'h2'=2,'h1'=2,'h0'=2,'lo'=2,'ep'=8] {'h3','h2','h1',..., dimensions={0}, use_global_device_ids=true | all-gather | bytes 313344 | tf_op jit(solution)/shard_map/all_gather | solution.py:150
  76.4 0.0 copy-start.1
  76.4 0.0 copy-start.2
  76.4 0.5 pack.1
  76.9 0.0 copy-start
  76.9 24.6 %all_to_all.15 = bf16[16,24,1920]{2,1,0:T(8,128)(2,1)S(1)} all-to-all(bf16[16,24,1920]{2,1,0:T(8,128)(2,1)S(1)} %bitcast.9), channel_id=1, replica_groups=mesh['rep'=2,'h3'=2,'h2'=2,'h1'=2,'h0'=2,'lo'=2,'ep'=8] {'lo','ep'}, dimensions={0} | all-to-all | bytes 2949120 | tf_op jit(solution)/shard_map/all_to_all | solution.py:160
  101.6 0.0 copy-done.1
  101.6 0.0 copy-done.2
  101.6 0.0 copy-done
  101.6 2.6 %ffn.1 = bf16[2,8,24,1920]{3,2,1,0:T(8,128)(2,1)S(1)} custom-call(bf16[2,8,24,1920]{3,2,1,0:T(8,128)(2,1)S(1)} %bitcast.10, bf16[16,2,96,256]{3,2,1,0:T(8,128)(2,1)S(1)} %bitcast.13, bf16[16,2,96,256]{3,2,1,0:T(8,128)(2,1)S(1)} %bitcast.14, bf16[256,3072]{1,0:T(8,128)(2,1)S(1)} %bitcast.15), custom_call_target="tpu_custom_call" | custom-call | tf_op jit(solution)/shard_map/ffn/pallas_call | solution.py:164
  104.2 0.0 copy-start.4
  104.2 23.8 %all_to_all.16.back_ref = bf16[16,24,1920]{2,1,0:T(8,128)(2,1)S(1)} all-to-all(bf16[16,24,1920]{2,1,0:T(8,128)(2,1)S(1)} %bitcast.11), channel_id=1, replica_groups=mesh['rep'=2,'h3'=2,'h2'=2,'h1'=2,'h0'=2,'lo'=2,'ep'=8] {'lo','ep'}, dimensions={0} | all-to-all | bytes 2949120 | tf_op jit(solution)/shard_map/all_to_all | solution.py:178
  127.9 0.0 copy-done.4
  127.9 0.8 combine.1
  128.7 46.3 %all_to_all.17.shares_ref = bf16[16,72,128]{2,1,0:T(8,128)(2,1)S(1)} all-to-all(bf16[16,72,128]{2,1,0:T(8,128)(2,1)S(1)} %combine.1), channel_id=1, replica_groups={{0,48,16,32,128,176,144,160,64,112,80,96,192,240,208,224},{8,56,24,40,1..., dimensions={0} | all-to-all | bytes 589824 | tf_op jit(solution)/shard_map/all_to_all | solution.py:190
  175.0 0.7 finish.1
Async XLA Ops:
  0.0 0.7 copy-start.3
  76.4 25.2 %copy-start.1 = (bf16[1,3072,256]{2,1,0:T(8,128)(2,1)S(1)}, bf16[1,3072,256]{2,1,0:T(8,128)(2,1)}, u32[]{:S(2)}) copy-start(bf16[1,3072,256]{2,1,0:T(8,128)(2,1)} %param.10) | copy-start | bytes 4718596
  76.4 25.2 %copy-start.2 = (bf16[1,256,3072]{2,1,0:T(8,128)(2,1)S(1)}, bf16[1,256,3072]{2,1,0:T(8,128)(2,1)}, u32[]{:S(2)}) copy-start(bf16[1,256,3072]{2,1,0:T(8,128)(2,1)} %param.11) | copy-start | bytes 4718596
  76.9 24.7 %copy-start = (bf16[1,3072,256]{2,1,0:T(8,128)(2,1)S(1)}, bf16[1,3072,256]{2,1,0:T(8,128)(2,1)}, u32[]{:S(2)}) copy-start(bf16[1,3072,256]{2,1,0:T(8,128)(2,1)} %param.9) | copy-start | bytes 4718596
  104.2 23.8 %copy-start.4 = (f32[96,2]{0,1:T(2,128)S(1)}, f32[96,2]{0,1:T(2,128)}, u32[]{:S(2)}) copy-start(f32[96,2]{0,1:T(2,128)} %param.8) | copy-start | bytes 2308
